TPU v7x, 8 devices: a whole 2x2x1 slice. The times are simulated.
8 devices in a mesh: dp: 2 (over z, y), sp: 4 (over x, core).
Axes of the slice: x: 2, y: 2, z: 1, core: 2. Of those that a mesh axis runs over, the one named last changes fastest.
Arguments:
- hidden: bfloat16 [128, 6144], P(('dp', 'sp')), parts along dimension 0
- w_q: bfloat16 [6144, 12288], replicated
- w_k: bfloat16 [6144, 1024], replicated
- w_v: bfloat16 [6144, 1024], replicated
- w_o: bfloat16 [12288, 6144], replicated
- expert_ids: int32 [128, 2], P(('dp', 'sp')), parts along dimension 0
- router_probs: float32 [128, 160], P(('dp', 'sp')), parts along dimension 0
Outputs:
- output 1: bfloat16 [128, 6144], P(('dp', 'sp')), parts along dimension 0
- output 2: bfloat16 [320, 64, 6144], P(('dp', 'sp')), parts along dimension 0
There are 2 independent parts. A program takes and returns all parts, laid end to end along the dimension named above; an argument that names none is the same for every part.
All inputs are finite; a program needn't handle non-finite values.
Results may differ from a plain program's by a relative error of at most 0.00846543.
Values are sent between devices in bfloat16 or wider.
A program may use at most 1.5 GiB of HBM per device.

v0:
```python
import math
import jax
import jax.numpy as jnp
from jax import lax
from jax.sharding import PartitionSpec as P

HEAD_DIM = 128
SCORE_SCALE = 1.0 / math.sqrt(HEAD_DIM)


def route_rows(hidden_out, expert_ids, router_probs):
    tok_dev, width = hidden_out.shape
    experts = router_probs.shape[1]
    picked = jnp.take_along_axis(router_probs, expert_ids, axis=1)
    gate_w = picked / jnp.sum(picked, axis=1, keepdims=True)
    gated = (gate_w[:, :, None] * hidden_out[:, None, :].astype(jnp.float32)).astype(jnp.bfloat16)
    token_hits = jnp.sum((expert_ids[:, :, None] == jnp.arange(experts)).astype(jnp.int32), axis=1)
    earlier = jnp.cumsum(token_hits, axis=0) - token_hits
    slot_rank = jnp.take_along_axis(earlier, expert_ids, axis=1)
    send_buf = jnp.zeros((experts, tok_dev, width), jnp.bfloat16)
    return send_buf.at[expert_ids, slot_rank].set(gated, unique_indices=True)


def solution(mesh):
    group = mesh.shape['sp']
    row_spec = P(('dp', 'sp'), None)
    buf_spec = P(('dp', 'sp'), None, None)

    def device_step(x_loc, w_q, w_k, w_v, w_o, ids_loc, probs_loc):
        tok_dev = x_loc.shape[0]
        seq_len = tok_dev * group
        n_heads = w_q.shape[1] // HEAD_DIM
        kv_heads = w_k.shape[1] // HEAD_DIM
        kv_copies = max(1, group // kv_heads)
        head_dev = n_heads // group
        kv_dev = kv_heads * kv_copies // group
        q_loc = jnp.dot(x_loc, w_q, preferred_element_type=jnp.float32).astype(jnp.bfloat16).reshape(tok_dev, n_heads, HEAD_DIM)
        k_loc = jnp.dot(x_loc, w_k, preferred_element_type=jnp.float32).astype(jnp.bfloat16).reshape(tok_dev, kv_heads, HEAD_DIM)
        v_loc = jnp.dot(x_loc, w_v, preferred_element_type=jnp.float32).astype(jnp.bfloat16).reshape(tok_dev, kv_heads, HEAD_DIM)
        k_loc = jnp.repeat(k_loc, kv_copies, axis=1)
        v_loc = jnp.repeat(v_loc, kv_copies, axis=1)
        q_seq = lax.all_to_all(q_loc, 'sp', 1, 0, tiled=True)
        k_seq = lax.all_to_all(k_loc, 'sp', 1, 0, tiled=True)
        v_seq = lax.all_to_all(v_loc, 'sp', 1, 0, tiled=True)
        q_grp = q_seq.reshape(seq_len, kv_dev, head_dev // kv_dev, HEAD_DIM)
        scores = jnp.einsum('qgmd,kgd->gmqk', q_grp, k_seq, preferred_element_type=jnp.float32) * SCORE_SCALE
        positions = jnp.arange(seq_len)
        causal = positions[:, None] >= positions[None, :]
        weights = jax.nn.softmax(jnp.where(causal, scores, -1e30), axis=-1).astype(jnp.bfloat16)
        attn_seq = jnp.einsum('gmqk,kgd->qgmd', weights, v_seq, preferred_element_type=jnp.float32).astype(jnp.bfloat16)
        attn_seq = attn_seq.reshape(seq_len, head_dev, HEAD_DIM)
        attn_loc = lax.all_to_all(attn_seq, 'sp', 0, 1, tiled=True).reshape(tok_dev, n_heads * HEAD_DIM)
        out_proj = jnp.dot(attn_loc, w_o, preferred_element_type=jnp.float32)
        hidden_out = (x_loc.astype(jnp.float32) + out_proj).astype(jnp.bfloat16)
        send_buf = route_rows(hidden_out, ids_loc, probs_loc)
        recv_buf = lax.all_to_all(send_buf, 'sp', 0, 1, tiled=True)
        return hidden_out, recv_buf

    return jax.shard_map(device_step, mesh=mesh, in_specs=(row_spec, P(), P(), P(), P(), row_spec, row_spec), out_specs=(row_spec, buf_spec), check_vma=False)
```

profile of v0, /device:TPU:0, one launch (start us, length us, event | category | flops | bytes accessed | tf_op | source)
XLA Modules:
  0.0 549.6 jit_solution(14226886048426911470)
XLA Ops:
  0.7 6.5 %fusion.8 = bf16[2,8,8,128]{3,2,1,0:T(8,128)(2,1)S(1)} fusion(bf16[16,6144]{1,0:T(8,128)(2,1)} %param.7, bf16[6144,1024]{1,0:T(8,128)(2,1)} %param.9), kind=kOutput, calls=%fused_computation.17 | convolution fusion | flops 201342976 | bytes 12812288 | tf_op jit(solution)/shard_map/dot_general | solution.py:38
  7.1 0.6 copy.125
  7.8 4.6 all-to-all-start.1
  12.4 6.4 %fusion.7 = bf16[2,8,8,128]{3,2,1,0:T(8,128)(2,1)S(1)} fusion(bf16[16,6144]{1,0:T(8,128)(2,1)} %param.7, bf16[6144,1024]{1,0:T(8,128)(2,1)} %param.10), kind=kOutput, calls=%fused_computation.16 | convolution fusion | flops 201342976 | bytes 12812288 | tf_op jit(solution)/shard_map/dot_general | solution.py:39
  18.8 48.0 %fusion.6 = bf16[2,96,8,128]{3,2,1,0:T(8,128)(2,1)S(1)} fusion(bf16[16,6144]{1,0:T(8,128)(2,1)S(1)} %copy-done.2, bf16[6144,12288]{1,0:T(8,128)(2,1)} %param.8), kind=kOutput, calls=%fused_computation.13 | convolution fusion | flops 2416115712 | bytes 151584768 | tf_op jit(solution)/shard_map/dot_general | solution.py:37
  66.8 0.1 copy.102
  66.9 0.1 reshape.52
  67.0 0.8 gather_fusion.1
  67.8 0.1 copy.105
  67.9 0.6 copy.126
  68.6 3.3 all-to-all-start
  71.9 0.8 copy.124
  72.7 2.9 all-to-all-done
  75.6 3.5 all-to-all-start.2
  79.1 0.1 copy.106
  79.2 7.0 %all-to-all-done.2 = bf16[16,96,128]{2,0,1:T(8,128)(2,1)S(1)} async-done(((bf16[16,96,128]{2,0,1:T(8,128)(2,1)}), bf16[16,96,128]{2,0,1:T(8,128)(2,1)S(1)}, u32[]{:S(2)}, u32[]{:S(2)}) %all-to-all-start.2) | async-done | bytes 393248 | tf_op jit(solution)/shard_map/all_to_all | solution.py:42
  86.3 0.5 fusion.18
  86.8 0.5 fusion.5
  87.3 0.4 convolution_convert_fusion.1
  87.7 1.0 copy.100
  88.7 3.6 all-to-all-start.3
  92.5 0.8 gather_fusion
  93.4 0.1 copy.104
  93.5 0.1 reshape.64
  93.6 5.7 %all-to-all-done.3 = bf16[64,24,128]{2,1,0:T(8,128)(2,1)S(1)} async-done(((bf16[64,24,128]{2,1,0:T(8,128)(2,1)}), bf16[64,24,128]{2,1,0:T(8,128)(2,1)S(1)}, u32[]{:S(2)}, u32[]{:S(2)}) %all-to-all-start.3) | async-done | bytes 393248 | tf_op jit(solution)/shard_map/all_to_all | solution.py:52
  99.4 48.7 %fusion.19 = (f32[16,6144]{1,0:T(8,128)S(1)}, bf16[16,6144]{1,0:T(8,128)(2,1)}) fusion(bf16[12288,6144]{1,0:T(8,128)(2,1)} %param.11, bf16[2,8,96,128]{3,2,1,0:T(8,128)(2,1)S(1)} %bitcast.87, bf16[16,6144]{1,0:T(8,128)(2,1)S(1)} %copy-done.2), kind=kOutput, calls=%fused_computation.45 | convolution fusion | flops 2416312320 | bytes 152174592 | tf_op jit(solution)/shard_map/dot_general | solution.py:53
  148.1 0.3 multiply_convert_fusion
  148.4 0.1 reshape.66
  148.6 10.5 %broadcast_in_dim.34 = bf16[160,16,6144]{2,1,0:T(8,128)(2,1)} broadcast(bf16[]{:T(256)} %constant.25.clone.1), dimensions={} | broadcast | bytes 31457282 | tf_op jit(solution)/shard_map/broadcast_in_dim | solution.py:20
  159.1 11.6 %scatter_fusion = bf16[160,16,6144]{2,1,0:T(8,128)(2,1)} fusion(bf16[160,16,6144]{2,1,0:T(8,128)(2,1)} %broadcast_in_dim.34, s32[32]{0:T(128)S(1)} %reshape.64, bf16[32,6144]{1,0:T(8,128)(2,1)S(1)} %reshape.66), kind=kCustom, calls=%fused_computation.2 | custom fusion | bytes 1179904 | tf_op jit(solution)/shard_map/scatter | solution.py:21
  170.7 357.3 %all_to_all.84 = bf16[160,16,6144]{2,1,0:T(8,128)(2,1)} all-to-all(bf16[160,16,6144]{2,1,0:T(8,128)(2,1)} %scatter_fusion), channel_id=1, replica_groups=mesh['dp'=2,'sp'=4] {'sp'}, dimensions={0} | all-to-all | bytes 62914560 | tf_op jit(solution)/shard_map/all_to_all | solution.py:56
  528.0 21.4 %copy.107 = bf16[40,4,16,6144]{3,2,1,0:T(8,128)(2,1)} copy(bf16[40,4,16,6144]{3,2,0,1:T(8,128)(2,1)} %bitcast.85) | data formatting | bytes 62914560 | tf_op jit(solution)/shard_map/all_to_all | solution.py:56
  (24 shorter events, 0.5 us)
Async XLA Ops:
  0.6 66.4 %copy-start = (f32[16,160]{1,0:T(8,128)S(1)}, f32[16,160]{1,0:T(8,128)}, u32[]{:S(2)}) copy-start(f32[16,160]{1,0:T(8,128)} %param.13) | copy-start | bytes 30724
  0.6 18.1 %copy-start.2 = (bf16[16,6144]{1,0:T(8,128)(2,1)S(1)}, bf16[16,6144]{1,0:T(8,128)(2,1)}, u32[]{:S(2)}) copy-start(bf16[16,6144]{1,0:T(8,128)(2,1)} %param.7) | copy-start | bytes 589828
  7.8 60.8 %all-to-all-start.1 = ((bf16[16,8,128]{2,0,1:T(8,128)(2,1)}), bf16[16,8,128]{2,0,1:T(8,128)(2,1)S(1)}, u32[]{:S(2)}, u32[]{:S(2)}) async-start(bf16[16,8,128]{2,0,1:T(8,128)(2,1)} %bitcast.82), calls=%async_computation.1 | async-start | bytes 65536 | tf_op jit(solution)/shard_map/all_to_all | solution.py:43
  18.8 48.0 %copy-start.3 = (s32[16,2]{0,1:T(2,128)S(1)}, s32[16,2]{0,1:T(2,128)}, u32[]{:S(2)}) copy-start(s32[16,2]{0,1:T(2,128)} %param.12) | copy-start | bytes 388
  68.6 7.0 %all-to-all-start = ((bf16[16,8,128]{2,0,1:T(8,128)(2,1)}), bf16[16,8,128]{2,0,1:T(8,128)(2,1)S(1)}, u32[]{:S(2)}, u32[]{:S(2)}) async-start(bf16[16,8,128]{2,0,1:T(8,128)(2,1)} %bitcast.83), calls=%async_computation | async-start | bytes 65536 | tf_op jit(solution)/shard_map/all_to_all | solution.py:44
  75.6 10.6 %all-to-all-start.2 = ((bf16[16,96,128]{2,0,1:T(8,128)(2,1)}), bf16[16,96,128]{2,0,1:T(8,128)(2,1)S(1)}, u32[]{:S(2)}, u32[]{:S(2)}) async-start(bf16[16,96,128]{2,0,1:T(8,128)(2,1)} %bitcast.81), calls=%async_computation.2 | async-start | bytes 786432 | tf_op jit(solution)/shard_map/all_to_all | solution.py:42
  88.7 10.6 %all-to-all-start.3 = ((bf16[64,24,128]{2,1,0:T(8,128)(2,1)}), bf16[64,24,128]{2,1,0:T(8,128)(2,1)S(1)}, u32[]{:S(2)}, u32[]{:S(2)}) async-start(bf16[64,24,128]{2,1,0:T(8,128)(2,1)} %copy.100), calls=%async_computation.3 | async-start | bytes 786432 | tf_op jit(solution)/shard_map/all_to_all | solution.py:52
  528.0 21.4 %copy-start.1 = (f32[16,160]{1,0:T(8,128)S(1)}, f32[16,160]{1,0:T(8,128)}, u32[]{:S(2)}) copy-start(f32[16,160]{1,0:T(8,128)} %param.13) | copy-start | bytes 30724
where the time goes:
time: 550 us
  blocking collectives  357 us (65%)
  matrix products  111 us (20%)
  local copies, waits for them, and re-layouts  49.2 us (9%)
  waiting for transfers between devices  15.7 us (3%)
  starting transfers between devices  15 us (3%)
    all_to_all x1, blocking collectives, device_step(): recv_buf = lax.all_to_all(send_buf, 'sp', 0, 1, tiled=True)  357 us
    dot_general x1, matrix products, device_step(): out_proj = jnp.dot(attn_loc, w_o, preferred_element_type=jnp.float32)  48.7 us
    dot_general x1, matrix products, device_step(): jnp.dot(x_loc, w_q, preferred_element_type=jnp.float32).astype(jnp.bfloat16)  48 us
    all_to_all x1, local copies, waits for them, and re-layouts, device_step(): recv_buf = lax.all_to_all(send_buf, 'sp', 0, 1, tiled=True)  21.4 us
    scatter x1, local copies, waits for them, and re-layouts, route_rows(): return send_buf.at[expert_ids, slot_rank].set(gated, unique_indices=True)  11.6 us
  transfers between devices with their start and end apart: 4, of which 3 were waited for; matrix products, arithmetic and copies ran while one was open for 11% of the time, Pallas kernels for 0%

commit v1 on v0

v1 whole, which is shorter than its diff:
```python
import functools
import math
import jax
import jax.numpy as jnp
from jax import lax
from jax.experimental import pallas as pl
from jax.experimental.pallas import tpu as pltpu
from jax.sharding import PartitionSpec as P

HEAD_DIM = 128
SCORE_SCALE = 1.0 / math.sqrt(HEAD_DIM)
SLOTS = 10
BLOCKS = 8
MESH = pl.DeviceIdType.MESH
ANY = pl.BlockSpec(memory_space=pl.ANY)
VMEM = pl.BlockSpec(memory_space=pltpu.VMEM)
SMEM = pl.BlockSpec(memory_space=pltpu.SMEM)


def peer_of(me, mask):
    chip = lax.rem(me // 2 + mask // 2, 2)
    core = lax.rem(lax.rem(me, 2) + mask % 2, 2)
    return chip * 2 + core


def attend_kernel(x_hbm, wq_hbm, wk_hbm, wv_hbm, wo_hbm, ids_ref, probs_ref, h_ref, meta_ref,
                  ring, wk_buf, wv_buf, x_all, o_all, m_all, acc, k_acc, v_acc,
                  w_sem, kv_sem, xl_sem, xs_snd, xs_rcv, xd_snd, xd_rcv, xf_snd, xf_rcv,
                  os_snd, os_rcv, od_snd, od_rcv, of_snd, of_rcv, m_snd, m_rcv):
    me = lax.axis_index('sp')
    tok = x_hbm.shape[0]
    seq = x_all.shape[1]
    wide = ring.shape[2]
    steps = x_all.shape[0]
    kv_w = wk_buf.shape[1]
    heads = wide // HEAD_DIM

    def weight_copy(src, slot):
        return pltpu.make_async_copy(src, ring.at[slot], w_sem.at[slot])

    def q_copy(kv, step, slot):
        rows = pl.ds(pl.multiple_of(step * wide, wide), wide)
        cols = pl.ds(pl.multiple_of((me * 2 + kv) * wide, wide), wide)
        return weight_copy(wq_hbm.at[rows, cols], slot)

    def o_copy(j, slot):
        dev = lax.rem(me // 2 + (j % 4) // 2, 2) * 2 + lax.rem(lax.rem(me, 2) + j % 2, 2)
        rows = pl.ds(pl.multiple_of((dev * 2 + j // 4) * wide, wide), wide)
        cols = pl.ds(pl.multiple_of(me * wide, wide), wide)
        return weight_copy(wo_hbm.at[rows, cols], slot)

    kv_cols = pl.ds(pl.multiple_of(me * kv_w, kv_w), kv_w)
    k_copy = pltpu.make_async_copy(wk_hbm.at[:, kv_cols], wk_buf, kv_sem.at[0])
    v_copy = pltpu.make_async_copy(wv_hbm.at[:, kv_cols], wv_buf, kv_sem.at[1])
    q_copy(0, 0, 0).start()
    k_copy.start()
    v_copy.start()
    for n in range(1, 8):
        q_copy(n // 4, n % 4, n).start()
    for n in range(8, SLOTS):
        o_copy(n - 8, n).start()

    mine = pl.ds(pl.multiple_of(me * tok, tok), tok)
    core_mate = peer_of(me, 1)
    chip_mate = peer_of(me, 2)

    def x_local(step):
        cols = pl.ds(pl.multiple_of(step * wide, wide), wide)
        return pltpu.make_async_copy(x_hbm.at[:, cols], x_all.at[step, mine], xl_sem.at[step])

    def x_send(step, to, snd, rcv):
        cols = pl.ds(pl.multiple_of(step * wide, wide), wide)
        return pltpu.make_async_remote_copy(
            src_ref=x_hbm.at[:, cols], dst_ref=x_all.at[step, mine], send_sem=snd.at[step],
            recv_sem=rcv.at[step], device_id={'sp': to}, device_id_type=MESH)

    def x_forward(step):
        theirs = pl.ds(pl.multiple_of(chip_mate * tok, tok), tok)
        return pltpu.make_async_remote_copy(
            src_ref=x_all.at[step, theirs], dst_ref=x_all.at[step, theirs], send_sem=xf_snd.at[step],
            recv_sem=xf_rcv.at[step], device_id={'sp': core_mate}, device_id_type=MESH)

    def o_send(slot, kv, to, snd, rcv):
        return pltpu.make_async_remote_copy(
            src_ref=o_all.at[slot], dst_ref=o_all.at[slot], send_sem=snd.at[kv],
            recv_sem=rcv.at[kv], device_id={'sp': to}, device_id_type=MESH)

    def m_send(mask):
        return pltpu.make_async_remote_copy(
            src_ref=m_all.at[mine], dst_ref=m_all.at[mine], send_sem=m_snd.at[mask],
            recv_sem=m_rcv.at[mask], device_id={'sp': peer_of(me, mask)}, device_id_type=MESH)

    for step in range(steps):
        x_local(step).start()
    barrier = pltpu.get_barrier_semaphore()
    for mask in (1, 2, 3):
        pl.semaphore_signal(barrier, inc=1, device_id={'sp': peer_of(me, mask)}, device_id_type=MESH)
    pl.semaphore_wait(barrier, 3)
    for step in range(steps):
        x_send(step, chip_mate, xs_snd, xs_rcv).start()
        x_send(step, core_mate, xd_snd, xd_rcv).start()

    ids = ids_ref[...]
    probs = probs_ref[...]
    lanes = lax.broadcasted_iota(jnp.int32, probs.shape, 1)
    p0 = jnp.sum(jnp.where(lanes == ids[:, 0:1], probs, 0.0), axis=1, keepdims=True)
    p1 = jnp.sum(jnp.where(lanes == ids[:, 1:2], probs, 0.0), axis=1, keepdims=True)
    total = p0 + p1
    cols = lax.broadcasted_iota(jnp.int32, (tok, HEAD_DIM), 1)
    fids = ids.astype(jnp.float32)
    meta = jnp.where(cols == 0, fids[:, 0:1], jnp.where(cols == 1, fids[:, 1:2],
           jnp.where(cols == 2, p0 / total, jnp.where(cols == 3, p1 / total, 0.0))))
    m_all[mine, :] = meta
    for mask in (1, 2, 3):
        m_send(mask).start()

    acc[...] = jnp.zeros_like(acc)
    k_acc[...] = jnp.zeros_like(k_acc)
    v_acc[...] = jnp.zeros_like(v_acc)

    def first_step(step, carry):
        x_send(step, chip_mate, xs_snd, xs_rcv).wait_recv()
        x_forward(step).start()
        x_local(step).wait()
        x_send(step, core_mate, xd_snd, xd_rcv).wait_recv()
        x_forward(step).wait_recv()

        @pl.when(step == 0)
        def _():
            k_copy.wait()
            v_copy.wait()

        x = x_all[step]
        rows = pl.ds(pl.multiple_of(step * wide, wide), wide)
        k_acc[...] += jnp.dot(x, wk_buf[rows, :], preferred_element_type=jnp.float32)
        v_acc[...] += jnp.dot(x, wv_buf[rows, :], preferred_element_type=jnp.float32)
        q_copy(0, step, step).wait()
        acc[...] += jnp.dot(x, ring[step], preferred_element_type=jnp.float32)
        o_copy(step + SLOTS - 8, step).start()
        return carry

    def second_step(step, carry):
        q_copy(1, step, 4 + step).wait()
        acc[...] += jnp.dot(x_all[step], ring[4 + step], preferred_element_type=jnp.float32)

        @pl.when(step < 12 - SLOTS)
        def _():
            o_copy(step + SLOTS - 4, 4 + step).start()
        return carry

    def attention(kv):
        q = acc[...].astype(jnp.bfloat16)
        k = k_acc[:, kv * HEAD_DIM:(kv + 1) * HEAD_DIM].astype(jnp.bfloat16)
        v = v_acc[:, kv * HEAD_DIM:(kv + 1) * HEAD_DIM].astype(jnp.bfloat16)
        q = jnp.concatenate([q[:, m * HEAD_DIM:(m + 1) * HEAD_DIM] for m in range(heads)], axis=0)
        s = lax.dot_general(q, k, (((1,), (1,)), ((), ())), preferred_element_type=jnp.float32) * SCORE_SCALE
        row = lax.rem(lax.broadcasted_iota(jnp.int32, s.shape, 0), seq)
        s = jnp.where(row >= lax.broadcasted_iota(jnp.int32, s.shape, 1), s, -1e30)
        e = jnp.exp(s - jnp.max(s, axis=1, keepdims=True))
        w = (e / jnp.sum(e, axis=1, keepdims=True)).astype(jnp.bfloat16)
        o = jnp.dot(w, v, preferred_element_type=jnp.float32).astype(jnp.bfloat16)
        slot = me * 2 + kv
        for m in range(heads):
            o_all[slot, :, m * HEAD_DIM:(m + 1) * HEAD_DIM] = o[m * seq:(m + 1) * seq]
        o_send(slot, kv, chip_mate, os_snd, os_rcv).start()
        o_send(slot, kv, core_mate, od_snd, od_rcv).start()

    lax.fori_loop(0, steps, first_step, 0)
    attention(0)
    acc[...] = jnp.zeros_like(acc)
    lax.fori_loop(0, steps, second_step, 0)
    attention(1)
    acc[...] = jnp.zeros_like(acc)

    def out_step(j, carry):
        kv = j // 4
        mask = lax.rem(j, 4)
        far = chip_mate * 2 + kv

        @pl.when(mask == 1)
        def _():
            o_send(far, kv, core_mate, od_snd, od_rcv).wait_recv()

        @pl.when(mask == 2)
        def _():
            o_send(far, kv, chip_mate, os_snd, os_rcv).wait_recv()
            o_send(far, kv, core_mate, of_snd, of_rcv).start()

        @pl.when(mask == 3)
        def _():
            o_send(far, kv, core_mate, of_snd, of_rcv).wait_recv()

        slot = lax.rem(8 + j, SLOTS)
        dev = lax.rem(me // 2 + mask // 2, 2) * 2 + lax.rem(lax.rem(me, 2) + lax.rem(mask, 2), 2)
        o_copy(0, slot).wait()
        acc[...] += jnp.dot(o_all[dev * 2 + kv], ring[slot], preferred_element_type=jnp.float32)
        return carry

    lax.fori_loop(0, 8, out_step, 0)
    h_ref[...] = (x_all[me].astype(jnp.float32) + acc[...]).astype(jnp.bfloat16)

    for mask in (1, 2, 3):
        m_send(mask).wait()
    meta_ref[...] = m_all[...]
    for step in range(steps):
        x_send(step, chip_mate, xs_snd, xs_rcv).wait_send()
        x_send(step, core_mate, xd_snd, xd_rcv).wait_send()
        x_forward(step).wait_send()
    for kv in range(2):
        o_send(0, kv, chip_mate, os_snd, os_rcv).wait_send()
        o_send(0, kv, core_mate, od_snd, od_rcv).wait_send()
        o_send(0, kv, core_mate, of_snd, of_rcv).wait_send()


def attend(x, w_q, w_k, w_v, w_o, ids, probs, group):
    tok, width = x.shape
    seq = tok * group
    kv_w = w_k.shape[1] // group
    kv_dev = kv_w // HEAD_DIM
    wide = w_q.shape[1] // group // kv_dev
    steps = width // wide
    f32, bf16 = jnp.float32, jnp.bfloat16
    dma = pltpu.SemaphoreType.DMA
    assert wide * group == width and kv_dev == 2 and group == 4
    return pl.pallas_call(
        attend_kernel,
        out_shape=(jax.ShapeDtypeStruct((seq, wide), bf16), jax.ShapeDtypeStruct((seq, HEAD_DIM), f32)),
        in_specs=[ANY] * 5 + [VMEM] * 2,
        out_specs=(VMEM, VMEM),
        scratch_shapes=[
            pltpu.VMEM((SLOTS, wide, wide), bf16),
            pltpu.VMEM((width, kv_w), bf16),
            pltpu.VMEM((width, kv_w), bf16),
            pltpu.VMEM((steps, seq, wide), bf16),
            pltpu.VMEM((group * 2, seq, wide), bf16),
            pltpu.VMEM((seq, HEAD_DIM), f32),
            pltpu.VMEM((seq, wide), f32),
            pltpu.VMEM((seq, kv_w), f32),
            pltpu.VMEM((seq, kv_w), f32),
            dma((SLOTS,)), dma((2,)), dma((steps,)),
        ] + [dma((steps,))] * 6 + [dma((2,))] * 6 + [dma((4,))] * 2,
        compiler_params=pltpu.CompilerParams(
            collective_id=0, has_side_effects=True, vmem_limit_bytes=66_000_000),
        cost_estimate=pl.CostEstimate(flops=seq * 2 * width * wide * 4, bytes_accessed=82_000_000, transcendentals=0),
        name='attend',
    )(x, w_q, w_k, w_v, w_o, ids, probs)


def zero_kernel(meta_smem, meta_ref, buf_hbm, list_ref, prep_ref, zero, flag, sem):
    me = lax.axis_index('sp')
    experts = buf_hbm.shape[0]
    seq = meta_ref.shape[0]
    tok = seq // 4
    zero[...] = jnp.zeros_like(zero)

    def fill(e):
        return pltpu.make_async_copy(zero, buf_hbm.at[e], sem.at[e])

    lax.fori_loop(0, experts, lambda e, c: (fill(e).start(), c)[1], 0)

    meta = meta_ref[...]
    rows = meta.T
    t_col = lax.broadcasted_iota(jnp.int32, (seq, seq), 0)
    t_row = lax.broadcasted_iota(jnp.int32, (seq, seq), 1)
    before = (t_col < t_row) & (t_col // tok == t_row // tok)
    source = (lax.broadcasted_iota(jnp.int32, (1, seq), 1) // tok).astype(jnp.float32)
    for k in range(2):
        same = (meta[:, 0:1] == rows[k:k + 1, :]) | (meta[:, 1:2] == rows[k:k + 1, :])
        rank = jnp.sum(jnp.where(before & same, 1.0, 0.0), axis=0, keepdims=True)
        prep_ref[k:k + 1, :] = (rows[k:k + 1, :] * 4.0 + source) * tok + rank
    prep_ref[2:4, :] = rows[2:4, :]

    def clear(i, c):
        flag[i] = 0
        return c

    lax.fori_loop(0, experts * 4 + 1, clear, 0)

    def visit(p, count):
        t = p // 2
        e = meta_smem[t, lax.rem(p, 2)].astype(jnp.int32) - me * experts
        inside = (e >= 0) & (e < experts)
        b = jnp.where(inside, e * 4 + t // tok, experts * 4)
        fresh = inside & (flag[b] == 0)

        @pl.when(fresh)
        def _():
            flag[b] = 1
            list_ref[count] = b
        return count + fresh.astype(jnp.int32)

    list_ref[2 * seq] = lax.fori_loop(0, 2 * seq, visit, 0)
    lax.fori_loop(0, experts, lambda e, c: (fill(e).wait(), c)[1], 0)


def zero_fill(meta, experts, width):
    seq = meta.shape[0]
    return pl.pallas_call(
        zero_kernel,
        out_shape=(jax.ShapeDtypeStruct((experts, seq, width), jnp.bfloat16),
                   jax.ShapeDtypeStruct((2 * seq + 8,), jnp.int32),
                   jax.ShapeDtypeStruct((8, seq), jnp.float32)),
        in_specs=[SMEM, VMEM],
        out_specs=(ANY, SMEM, VMEM),
        scratch_shapes=[pltpu.VMEM((seq, width), jnp.bfloat16), pltpu.SMEM((experts * 4 + 8,), jnp.int32),
                        pltpu.SemaphoreType.DMA((experts,))],
        cost_estimate=pl.CostEstimate(flops=8_000_000_000, bytes_accessed=experts * seq * width * 2, transcendentals=0),
        name='zero_fill',
    )(meta, meta)


def rows_kernel(list_ref, prep_ref, h0, h1, h2, h3, buf_in, buf_hbm, out_ref, stage, sem):
    me = lax.axis_index('sp')
    experts = buf_hbm.shape[0]
    tok = out_ref.shape[0]
    seq, wide = h0.shape
    count = list_ref[2 * seq]
    batches = (count + BLOCKS - 1) // BLOCKS
    parts = [(h, pl.ds(pl.multiple_of(peer_of(me, mask) * wide, wide), wide)) for mask, h in enumerate((h0, h1, h2, h3))]
    mine = pl.ds(pl.multiple_of(me * tok, tok), tok)
    for h, cols in parts:
        out_ref[:, cols] = h[mine, :]

    def put(batch, i):
        slot = lax.rem(batch, 2)
        b = list_ref[batch * BLOCKS + i]
        dst = pl.ds(pl.multiple_of(lax.rem(b, 4) * tok, tok), tok)
        return pltpu.make_async_copy(stage.at[slot, pl.ds(i * tok, tok)], buf_hbm.at[b // 4, dst], sem.at[slot, i])

    def drain(batch):
        for i in range(BLOCKS):
            @pl.when(batch * BLOCKS + i < count)
            def _():
                put(batch, i).wait()

    row = lax.broadcasted_iota(jnp.int32, (BLOCKS * tok, 1), 0)

    def batch_step(batch, carry):
        @pl.when(batch >= 2)
        def _():
            drain(batch - 2)

        key = jnp.zeros((BLOCKS * tok, 1), jnp.int32)
        for i in range(BLOCKS):
            key = jnp.where(row // tok == i, list_ref[batch * BLOCKS + i], key)
        key = ((key + me * experts * 4) * tok + lax.rem(row, tok)).astype(jnp.float32)
        hit0 = key == prep_ref[0:1, :]
        hit1 = key == prep_ref[1:2, :]
        gate = jnp.sum(jnp.where(hit0, prep_ref[2:3, :], 0.0) + jnp.where(hit1, prep_ref[3:4, :], 0.0),
                       axis=1, keepdims=True)
        pick = jnp.where(hit0 | hit1, 1.0, 0.0).astype(jnp.bfloat16)
        for h, cols in parts:
            rows = jnp.dot(pick, h[...], preferred_element_type=jnp.float32)
            stage[lax.rem(batch, 2), :, cols] = (gate * rows).astype(jnp.bfloat16)
        for i in range(BLOCKS):
            @pl.when(batch * BLOCKS + i < count)
            def _():
                put(batch, i).start()
        return carry

    lax.fori_loop(0, batches, batch_step, 0)

    @pl.when(batches >= 2)
    def _():
        drain(batches - 2)

    @pl.when(batches >= 1)
    def _():
        drain(batches - 1)


def write_rows(blocks, prep, hs, buf):
    experts, seq, width = buf.shape
    tok = seq // 4
    return pl.pallas_call(
        rows_kernel,
        out_shape=(jax.ShapeDtypeStruct(buf.shape, buf.dtype), jax.ShapeDtypeStruct((tok, width), jnp.bfloat16)),
        in_specs=[SMEM] + [VMEM] * 5 + [ANY],
        out_specs=(ANY, VMEM),
        input_output_aliases={6: 0},
        scratch_shapes=[pltpu.VMEM((2, BLOCKS * tok, width), jnp.bfloat16), pltpu.SemaphoreType.DMA((2, BLOCKS))],
        cost_estimate=pl.CostEstimate(flops=2_000_000_000, bytes_accessed=4_000_000, transcendentals=0),
        name='write_rows',
    )(blocks, prep, *hs, buf)


def solution(mesh):
    group = mesh.shape['sp']
    row_spec = P(('dp', 'sp'), None)
    buf_spec = P(('dp', 'sp'), None, None)

    def device_step(x_loc, w_q, w_k, w_v, w_o, ids_loc, probs_loc):
        experts = probs_loc.shape[1] // group
        h0, meta = attend(x_loc, w_q, w_k, w_v, w_o, ids_loc, probs_loc, group)
        swap = lambda mask: [(i, i ^ mask) for i in range(group)]
        h2 = lax.ppermute(h0, 'sp', swap(2))
        h1 = lax.ppermute(h0, 'sp', swap(1))
        h3 = lax.ppermute(h0, 'sp', swap(3))
        buf, blocks, prep = zero_fill(meta, experts, x_loc.shape[1])
        buf, hidden_out = write_rows(blocks, prep, (h0, h1, h2, h3), buf)
        return hidden_out, buf

    return jax.shard_map(device_step, mesh=mesh, in_specs=(row_spec, P(), P(), P(), P(), row_spec, row_spec), out_specs=(row_spec, buf_spec), check_vma=False)
```

time: 550 us -> 62.5 us (0.11)
  blocking collectives: 357 us -> 0 us
  matrix products: 111 us -> 0 us
  Pallas kernels: 0 us -> 57.4 us
  local copies, waits for them, and re-layouts: 49.2 us -> 2.14 us
  waiting for transfers between devices: 15.7 us -> 0.01 us
  starting transfers between devices: 15 us -> 2.05 us
    all_to_all x1 -> x0, blocking collectives: 357 us -> none  [device_step(): recv_buf = lax.all_to_all(send_buf, 'sp', 0, 1, tiled=True)]
    dot_general x6 -> x0, matrix products: 110 us -> none  [the longest x1 48.7 us: device_step(): out_proj = jnp.dot(attn_loc, w_o, preferred_element_type=jnp.float32)]
    pallas_call x0 -> x3, Pallas kernels: none -> 57.4 us  [the longest x1 40.8 us: attend(): pl.pallas_call(attend_kernel, out_shape=(jax.ShapeDtypeStruct((seq, wide)...]
    all_to_all x5 -> x0, local copies, waits for them, and re-layouts: 21.5 us -> none  [the longest x1 21.4 us: device_step(): recv_buf = lax.all_to_all(send_buf, 'sp', 0, 1, tiled=True)]
    all_to_all x4 -> x0, waiting for transfers between devices: 15.7 us -> none  [the longest x1 7.03 us: device_step(): q_seq = lax.all_to_all(q_loc, 'sp', 1, 0, tiled=True)]
    all_to_all x4 -> x0, starting transfers between devices: 15 us -> none  [the longest x1 4.61 us: device_step(): k_seq = lax.all_to_all(k_loc, 'sp', 1, 0, tiled=True)]
    scatter x1 -> x0, local copies, waits for them, and re-layouts: 11.6 us -> none  [route_rows(): return send_buf.at[expert_ids, slot_rank].set(gated, unique_indices=True)]
    broadcast_in_dim x1 -> x0, local copies, waits for them, and re-layouts: 10.5 us -> none  [route_rows(): send_buf = jnp.zeros((experts, tok_dev, width), jnp.bfloat16)]
  transfers between devices with their start and end apart: 4 -> 3, of which waited for: 3 -> 0; matrix products, arithmetic and copies ran while one was open for 11% -> 0% of each run, Pallas kernels for 0% -> 20%
where the time goes in v1:
time: 62.5 us; the launch traced here: 62.3 us
  Pallas kernels  57.4 us (92%)
  local copies, waits for them, and re-layouts  2.14 us (3%)
  starting transfers between devices  2.05 us (3%)
  between operations  0.7 us (1%)
    pallas_call x1, Pallas kernels, attend(): pl.pallas_call(attend_kernel, out_shape=(jax.ShapeDtypeStruct((seq, wide)...  40.8 us
    pallas_call x1, Pallas kernels, zero_fill(): pl.pallas_call(zero_kernel, out_shape=(jax.ShapeDtypeStruct((experts, seq...  12.4 us
    pallas_call x1, Pallas kernels, write_rows(): pl.pallas_call(rows_kernel, out_shape=(jax.ShapeDtypeStruct(buf.shape, bu...  4.18 us
    unnamed x7, local copies, waits for them, and re-layouts  2.14 us
    ppermute x1, starting transfers between devices, device_step(): h2 = lax.ppermute(h0, 'sp', swap(2))  1.32 us
  transfers between devices with their start and end apart: 3, of which 0 were waited for; matrix products, arithmetic and copies ran while one was open for 0% of the time, Pallas kernels for 20%

profile of v1, /device:TPU:0, one launch (start us, length us, event | category | flops | bytes accessed | tf_op | source)
XLA Modules:
  0.0 62.3 jit_solution(3704763735344098288)
XLA Ops:
  0.6 1.4 %copy.10.ids_ref = s32[16,2]{1,0:T(8,128)} copy(s32[16,2]{0,1:T(2,128)} %param.12) | data formatting | bytes 256 | tf_op args[5]
  2.0 40.8 %attend.1 = (bf16[64,1536]{1,0:T(8,128)(2,1)}, f32[64,128]{1,0:T(8,128)}) custom-call(bf16[16,6144]{1,0:T(8,128)(2,1)} %x_hbm.1, bf16[6144,12288]{1,0:T(8,128)(2,1)} %wq_hbm.1, bf16[6144,1024]{1,0:T(8,128)(2,1)} %wk_hbm.1, bf16[6144,1024]{1,0:T(8,128)(2,1)} %wv_hbm.1, bf16[12288,6144]{1,0:T(8,128)(2,1)} %wo_hbm.1, s32[16,2]{1,0:T(8,128)} %copy.10.ids_ref, ...), custom_call_target="tpu_custom_call" | custom-call | flops 4831838208 | bytes 82000000 | tf_op jit(solution)/shard_map/attend/pallas_call | solution.py:225
  42.8 0.7 %collective-permute-start.2 = (bf16[64,1536]{1,0:T(8,128)(2,1)}, bf16[64,1536]{1,0:T(8,128)(2,1)S(1)}, u32[]{:S(2)}, u32[]{:S(2)}) collective-permute-start(bf16[64,1536]{1,0:T(8,128)(2,1)} %get-tuple-element.12.h0), channel_id=1, source_target_pairs={{0,3},{1,2},{2,1},{3,0},{4,7},{5,6},{6,5},{7,4}} | collective-permute-start | bytes 589832 | tf_op jit(solution)/shard_map/ppermute | solution.py:398
  43.5 1.3 %collective-permute-start.1 = (bf16[64,1536]{1,0:T(8,128)(2,1)}, bf16[64,1536]{1,0:T(8,128)(2,1)S(1)}, u32[]{:S(2)}, u32[]{:S(2)}) collective-permute-start(bf16[64,1536]{1,0:T(8,128)(2,1)} %get-tuple-element.12.h0), channel_id=1, source_target_pairs={{0,2},{1,3},{2,0},{3,1},{4,6},{5,7},{6,4},{7,5}} | collective-permute-start | bytes 589832 | tf_op jit(solution)/shard_map/ppermute | solution.py:396
  44.9 0.0 collective-permute-start
  44.9 12.4 %zero_fill.1 = (bf16[40,64,6144]{2,1,0:T(8,128)(2,1)}, s32[136]{0:T(256)}, f32[8,64]{1,0:T(8,128)}) custom-call(f32[64,128]{1,0:T(8,128)} %get-tuple-element.9.meta_smem.meta_ref, f32[64,128]{1,0:T(8,128)} %get-tuple-element.9.meta_smem.meta_ref), custom_call_target="tpu_custom_call" | custom-call | flops 8000000000 | bytes 31457280 | tf_op jit(solution)/shard_map/zero_fill/pallas_call | solution.py:298
  57.3 0.0 collective-permute-done.2.h3
  57.3 0.0 copy-start
  57.3 0.0 collective-permute-done.1.h2
  57.3 0.0 copy-start.1
  57.3 0.0 collective-permute-done.h1
  57.3 0.0 copy-start.2
  57.3 0.6 %copy-done = bf16[64,1536]{1,0:T(8,128)(2,1)} copy-done((bf16[64,1536]{1,0:T(8,128)(2,1)}, bf16[64,1536]{1,0:T(8,128)(2,1)S(1)}, u32[]{:S(2)}) %copy-start) | copy-done | bytes 196632
  58.0 0.1 copy-done.1
  58.1 0.1 copy-done.2
  58.1 4.2 %write_rows.1 = (bf16[40,64,6144]{2,1,0:T(8,128)(2,1)}, bf16[16,6144]{1,0:T(8,128)(2,1)}) custom-call(s32[136]{0:T(256)} %get-tuple-element.10.list_ref, f32[8,64]{1,0:T(8,128)} %get-tuple-element.11.prep_ref, bf16[64,1536]{1,0:T(8,128)(2,1)} %get-tuple-element.12.h0, bf16[64,1536]{1,0:T(8,128)(2,1)} %copy-done.2, ...), custom_call_target="tpu_custom_call", output_to_operand_aliasing={{0}: (6, {})} | custom-call | flops 2000000000 | bytes 4000000 | tf_op jit(solution)/shard_map/write_rows/pallas_call | solution.py:375
Async XLA Ops:
  42.8 14.5 %collective-permute-start.2 = (bf16[64,1536]{1,0:T(8,128)(2,1)}, bf16[64,1536]{1,0:T(8,128)(2,1)S(1)}, u32[]{:S(2)}, u32[]{:S(2)}) collective-permute-start(bf16[64,1536]{1,0:T(8,128)(2,1)} %get-tuple-element.12.h0), channel_id=1, source_target_pairs={{0,3},{1,2},{2,1},{3,0},{4,7},{5,6},{6,5},{7,4}} | collective-permute-start | bytes 589832 | tf_op jit(solution)/shard_map/ppermute | solution.py:398
  43.5 13.8 %collective-permute-start.1 = (bf16[64,1536]{1,0:T(8,128)(2,1)}, bf16[64,1536]{1,0:T(8,128)(2,1)S(1)}, u32[]{:S(2)}, u32[]{:S(2)}) collective-permute-start(bf16[64,1536]{1,0:T(8,128)(2,1)} %get-tuple-element.12.h0), channel_id=1, source_target_pairs={{0,2},{1,3},{2,0},{3,1},{4,6},{5,7},{6,4},{7,5}} | collective-permute-start | bytes 589832 | tf_op jit(solution)/shard_map/ppermute | solution.py:396
  44.9 12.5 %collective-permute-start = (bf16[64,1536]{1,0:T(8,128)(2,1)}, bf16[64,1536]{1,0:T(8,128)(2,1)S(1)}, u32[]{:S(2)}, u32[]{:S(2)}) collective-permute-start(bf16[64,1536]{1,0:T(8,128)(2,1)} %get-tuple-element.12.h0), channel_id=1, source_target_pairs={{0,1},{1,0},{2,3},{3,2},{4,5},{5,4},{6,7},{7,6}} | collective-permute-start | bytes 589832 | tf_op jit(solution)/shard_map/ppermute | solution.py:397
  57.3 0.7 %copy-start = (bf16[64,1536]{1,0:T(8,128)(2,1)}, bf16[64,1536]{1,0:T(8,128)(2,1)S(1)}, u32[]{:S(2)}) copy-start(bf16[64,1536]{1,0:T(8,128)(2,1)S(1)} %collective-permute-done.2.h3) | copy-start | bytes 589828
  57.3 0.8 %copy-start.1 = (bf16[64,1536]{1,0:T(8,128)(2,1)}, bf16[64,1536]{1,0:T(8,128)(2,1)S(1)}, u32[]{:S(2)}) copy-start(bf16[64,1536]{1,0:T(8,128)(2,1)S(1)} %collective-permute-done.1.h2) | copy-start | bytes 589828
  57.3 0.8 %copy-start.2 = (bf16[64,1536]{1,0:T(8,128)(2,1)}, bf16[64,1536]{1,0:T(8,128)(2,1)S(1)}, u32[]{:S(2)}) copy-start(bf16[64,1536]{1,0:T(8,128)(2,1)S(1)} %collective-permute-done.h1) | copy-start | bytes 589828

commit v2 on v0

v2 whole, which is shorter than its diff:
```python
import math
import jax
import jax.numpy as jnp
from jax import lax
from jax.experimental import pallas as pl
from jax.experimental.pallas import tpu as pltpu
from jax.sharding import PartitionSpec as P

HEAD_DIM = 128
SCORE_SCALE = 1.0 / math.sqrt(HEAD_DIM)
SLOTS = 10
PARTS = ((0, 768), (768, 512), (1280, 256))
BLOCKS = 8
OCC = 256
EARLY = 4
MESH = pl.DeviceIdType.MESH
ANY = pl.BlockSpec(memory_space=pl.ANY)
VMEM = pl.BlockSpec(memory_space=pltpu.VMEM)
SMEM = pl.BlockSpec(memory_space=pltpu.SMEM)
F32, BF16 = jnp.float32, jnp.bfloat16


def peer_of(me, mask):
    chip = lax.rem(me // 2 + mask // 2, 2)
    core = lax.rem(lax.rem(me, 2) + mask % 2, 2)
    return chip * 2 + core


def span(start, size):
    return pl.ds(pl.multiple_of(start, size), size)


def dot(a, b):
    return jnp.dot(a, b, preferred_element_type=F32)


def attend_kernel(x_hbm, ids_hbm, probs_hbm, wq_hbm, wk_hbm, wv_hbm, wo_hbm, h_hbm, occ_hbm, prep_hbm,
                  ring, kv_buf, x_all, o_all, m_all, h_all, acc, kv_acc, q_ref, kv_ref, x_ref, ids_ref, probs_ref,
                  occ_ref, prep_ref, w_sem, kv_sem, p_sem, in_sem, out_sem, xs_snd, xs_rcv, xd_snd, xd_rcv, xf_snd, xf_rcv,
                  os_snd, os_rcv, od_snd, od_rcv, of_snd, of_rcv, hs_snd, hs_rcv, hd_snd, hd_rcv, hf_snd, hf_rcv,
                  m_snd, m_rcv):
    me = lax.axis_index('sp')
    tok, width = x_ref.shape
    seq = x_all.shape[0]
    wide = ring.shape[1]
    steps = width // wide
    kv_w = kv_buf.shape[1] // 2
    heads = wide // HEAD_DIM
    experts = probs_ref.shape[1] // 4
    core_mate = peer_of(me, 1)
    chip_mate = peer_of(me, 2)
    mine = span(me * tok, tok)
    theirs = span(chip_mate * tok, tok)

    def q_copy(n):
        return pltpu.make_async_copy(
            wq_hbm.at[span(lax.rem(n, 4) * wide, wide), span((me * 2 + n // 4) * wide, wide)],
            ring.at[span(n * wide, wide)], w_sem.at[n])

    def k_copy(c):
        rows = span(c * wide, wide)
        return pltpu.make_async_copy(wk_hbm.at[rows, span(me * kv_w, kv_w)], kv_buf.at[rows, pl.ds(0, kv_w)], kv_sem.at[0, c])

    def v_copy(c):
        rows = span(c * wide, wide)
        return pltpu.make_async_copy(wv_hbm.at[rows, span(me * kv_w, kv_w)], kv_buf.at[rows, pl.ds(kv_w, kv_w)], kv_sem.at[1, c])

    def o_copy(j):
        slot = (8 + j) % SLOTS
        return pltpu.make_async_copy(
            wo_hbm.at[span(peer_of(me, j) * 2 * wide, wide), span(me * wide, wide)],
            ring.at[pl.ds(slot * wide, wide)], w_sem.at[slot])

    def p_copy(p, r):
        off, size = PARTS[p]
        return pltpu.make_async_copy(
            wo_hbm.at[span((peer_of(me, r) * 2 + 1) * wide, wide), pl.ds(pl.multiple_of(me * wide + off, 256), size)],
            ring.at[pl.ds((2 + r) * wide, wide), pl.ds(off, size)], p_sem.at[p, r])

    def remote(src, dst, snd, rcv, to):
        return pltpu.make_async_remote_copy(src_ref=src, dst_ref=dst, send_sem=snd, recv_sem=rcv,
                                            device_id={'sp': to}, device_id_type=MESH)

    def x_far(c):
        cols = pl.ds(c * wide, wide)
        return remote(x_ref.at[:, cols], x_all.at[mine, cols], xs_snd.at[c], xs_rcv.at[c], chip_mate)

    def x_near(c):
        cols = pl.ds(c * wide, wide)
        return remote(x_ref.at[:, cols], x_all.at[mine, cols], xd_snd.at[c], xd_rcv.at[c], core_mate)

    def x_pass(c):
        cols = pl.ds(c * wide, wide)
        return remote(x_all.at[theirs, cols], x_all.at[theirs, cols], xf_snd.at[c], xf_rcv.at[c], core_mate)

    def o_part(kv, r):
        return o_all.at[kv, :, pl.ds(r * wide, wide)]

    def o_far(kv):
        return remote(o_part(kv, 0), o_part(kv, 2), os_snd.at[kv], os_rcv.at[kv], chip_mate)

    def o_near(kv):
        return remote(o_part(kv, 0), o_part(kv, 1), od_snd.at[kv], od_rcv.at[kv], core_mate)

    def o_pass(kv):
        return remote(o_part(kv, 2), o_part(kv, 3), of_snd.at[kv], of_rcv.at[kv], core_mate)

    def h_part(p, dev):
        off, size = PARTS[p]
        return h_all.at[:, pl.ds(pl.multiple_of(dev * wide + off, 256), size)]

    def h_far(p):
        return remote(h_part(p, me), h_part(p, me), hs_snd.at[p], hs_rcv.at[p], chip_mate)

    def h_near(p):
        return remote(h_part(p, me), h_part(p, me), hd_snd.at[p], hd_rcv.at[p], core_mate)

    def h_pass(p):
        return remote(h_part(p, chip_mate), h_part(p, chip_mate), hf_snd.at[p], hf_rcv.at[p], core_mate)

    def m_send(mask):
        return remote(m_all.at[mine], m_all.at[mine], m_snd.at[mask], m_rcv.at[mask], peer_of(me, mask))

    barrier = pltpu.get_barrier_semaphore()
    for mask in (1, 2, 3):
        pl.semaphore_signal(barrier, inc=1, device_id={'sp': peer_of(me, mask)}, device_id_type=MESH)
    x_in = pltpu.make_async_copy(x_hbm, x_ref, in_sem.at[0])
    ids_in = pltpu.make_async_copy(ids_hbm, ids_ref, in_sem.at[1])
    probs_in = pltpu.make_async_copy(probs_hbm, probs_ref, in_sem.at[2])
    x_in.start()
    ids_in.start()
    probs_in.start()

    def start_first(c, carry):
        q_copy(c).start()
        k_copy(c).start()
        v_copy(c).start()
        return carry

    def start_second(n, carry):
        q_copy(n).start()
        return carry

    lax.fori_loop(0, 4, start_first, 0)
    lax.fori_loop(4, 8, start_second, 0)
    o_copy(0).start()
    o_copy(1).start()
    x_in.wait()
    pl.semaphore_wait(barrier, 3)
    for c in range(steps):
        x_far(c).start()
        x_near(c).start()
    x_all[mine, :] = x_ref[...]
    ids_in.wait()
    probs_in.wait()
    ids = ids_ref[...].astype(F32)
    probs = probs_ref[...]
    eye = lax.broadcasted_iota(jnp.int32, (tok, tok), 0) == lax.broadcasted_iota(jnp.int32, (tok, tok), 1)
    id0 = jnp.sum(jnp.where(eye, ids[0:1, :], 0.0), axis=1, keepdims=True)
    id1 = jnp.sum(jnp.where(eye, ids[1:2, :], 0.0), axis=1, keepdims=True)
    lanes = lax.broadcasted_iota(jnp.int32, probs.shape, 1).astype(F32)
    p0 = jnp.sum(jnp.where(lanes == id0, probs, 0.0), axis=1, keepdims=True)
    p1 = jnp.sum(jnp.where(lanes == id1, probs, 0.0), axis=1, keepdims=True)
    total = p0 + p1
    cols = lax.broadcasted_iota(jnp.int32, (tok, HEAD_DIM), 1)
    m_all[mine, :] = jnp.where(cols == 0, id0, jnp.where(cols == 1, id1,
                     jnp.where(cols == 2, p0 / total, jnp.where(cols == 3, p1 / total, 0.0))))
    for mask in (1, 2, 3):
        m_send(mask).start()
    def first_dots(c):
        x_near(c).wait_recv()
        x_pass(c).wait_recv()
        k_copy(c).wait()
        v_copy(c).wait()
        x = x_all[:, c * wide:(c + 1) * wide]
        part = dot(x, kv_buf[c * wide:(c + 1) * wide, :])
        if c == 0:
            kv_acc[...] = part
        else:
            kv_acc[...] += part
        q_copy(c).wait()
        part = dot(x, ring[c * wide:(c + 1) * wide, :])
        if c == 0:
            acc[...] = part
        else:
            acc[...] += part

    for c in range(steps):
        x_far(c).wait_recv()
        x_pass(c).start()
        if c > 0:
            first_dots(c - 1)
    first_dots(steps - 1)

    def attention(kv):
        k = kv_ref[:, kv * HEAD_DIM:(kv + 1) * HEAD_DIM]
        v = kv_ref[:, kv_w + kv * HEAD_DIM:kv_w + (kv + 1) * HEAD_DIM]
        q = jnp.concatenate([q_ref[:, m * HEAD_DIM:(m + 1) * HEAD_DIM] for m in range(heads)], axis=0)
        s = lax.dot_general(q, k, (((1,), (1,)), ((), ())), preferred_element_type=F32) * SCORE_SCALE
        row = lax.rem(lax.broadcasted_iota(jnp.int32, s.shape, 0), seq)
        s = jnp.where(row >= lax.broadcasted_iota(jnp.int32, s.shape, 1), s, -1e30)
        e = jnp.exp(s - jnp.max(s, axis=1, keepdims=True))
        w = (e / jnp.sum(e, axis=1, keepdims=True)).astype(BF16)
        o = dot(w, v).astype(BF16)
        for m in range(heads):
            o_all[kv, :, m * HEAD_DIM:(m + 1) * HEAD_DIM] = o[m * seq:(m + 1) * seq]
        o_far(kv).start()
        o_near(kv).start()

    kv_ref[...] = kv_acc[...].astype(BF16)
    q_ref[...] = acc[...].astype(BF16)
    o_copy(2).start()
    o_copy(3).start()
    p_copy(0, 0).start()
    p_copy(0, 1).start()
    attention(0)

    q_copy(4).wait()
    q_copy(5).wait()
    acc[...] = dot(x_all[:, :2 * wide], ring[4 * wide:6 * wide, :])
    p_copy(0, 2).start()
    p_copy(0, 3).start()
    q_copy(6).wait()
    q_copy(7).wait()
    q_ref[...] = (acc[...] + dot(x_all[:, 2 * wide:], ring[6 * wide:8 * wide, :])).astype(BF16)
    for r in range(4):
        p_copy(1, r).start()
    attention(1)

    def routing():
        for mask in (1, 2, 3):
            m_send(mask).wait_recv()
        meta = m_all[...]
        rows = meta.T
        t_col = lax.broadcasted_iota(jnp.int32, (seq, seq), 0)
        t_row = lax.broadcasted_iota(jnp.int32, (seq, seq), 1)
        before = (t_col < t_row) & (t_col // tok == t_row // tok)
        source = (lax.broadcasted_iota(jnp.int32, (1, seq), 1) // tok).astype(F32)
        for k in range(2):
            same = (meta[:, 0:1] == rows[k:k + 1, :]) | (meta[:, 1:2] == rows[k:k + 1, :])
            rank = jnp.sum(jnp.where(before & same, 1.0, 0.0), axis=0, keepdims=True)
            prep_ref[k:k + 1, :] = (rows[k:k + 1, :] * 4.0 + source) * tok + rank
        prep_ref[2:4, :] = rows[2:4, :]
        prep_ref[4:8, :] = jnp.zeros((4, seq), F32)
        block = (lax.broadcasted_iota(jnp.int32, (seq, OCC), 1) + me * experts * 4).astype(F32)
        origin = (lax.broadcasted_iota(jnp.int32, (seq, 1), 0) // tok).astype(F32)
        used = (meta[:, 0:1] * 4.0 + origin == block) | (meta[:, 1:2] * 4.0 + origin == block)
        occ_ref[...] = jnp.max(jnp.where(used, 1, 0), axis=0, keepdims=True)
        occ_out = pltpu.make_async_copy(occ_ref, occ_hbm, out_sem.at[0])
        prep_out = pltpu.make_async_copy(prep_ref, prep_hbm, out_sem.at[1])
        occ_out.start()
        prep_out.start()
        return occ_out, prep_out

    for r in range(4):
        if r == 1:
            o_near(0).wait_recv()
            occ_out, prep_out = routing()
        if r == 2:
            o_far(0).wait_recv()
            o_pass(0).start()
        if r == 3:
            o_pass(0).wait_recv()
        o_copy(r).wait()
        if r == 0:
            for s in range(4):
                p_copy(2, s).start()
        slot = (8 + r) % SLOTS
        part = dot(o_all[0, :, r * wide:(r + 1) * wide], ring[slot * wide:(slot + 1) * wide, :])
        if r == 0:
            acc[...] = part
        else:
            acc[...] += part

    for p, (off, size) in enumerate(PARTS):
        cut = slice(off, off + size)
        if p == 0:
            o_near(1).wait_recv()
        p_copy(p, 0).wait()
        p_copy(p, 1).wait()
        part = dot(o_all[1, :, :2 * wide], ring[2 * wide:4 * wide, cut])
        acc[:, cut] += part
        if p == 0:
            o_far(1).wait_recv()
            o_pass(1).start()
            p_copy(p, 2).wait()
            part = dot(o_all[1, :, 2 * wide:3 * wide], ring[4 * wide:5 * wide, cut])
            acc[:, cut] += part
            o_pass(1).wait_recv()
            p_copy(p, 3).wait()
            part = dot(o_all[1, :, 3 * wide:], ring[5 * wide:6 * wide, cut])
        else:
            p_copy(p, 2).wait()
            p_copy(p, 3).wait()
            part = dot(o_all[1, :, 2 * wide:], ring[4 * wide:6 * wide, cut])
        home = pl.ds(pl.multiple_of(me * wide + off, 256), size)
        h_all[:, home] = (x_all[:, home].astype(F32) + (acc[:, cut] + part)).astype(BF16)
        h_far(p).start()
        h_near(p).start()

    last = PARTS[-1][0]

    def h_out(dev, off, size, sem):
        cut = pl.ds(dev * wide + off, size)
        return pltpu.make_async_copy(h_all.at[:, cut], h_hbm.at[:, cut], sem)

    for p in range(len(PARTS)):
        h_far(p).wait_recv()
        h_pass(p).start()
        if p > 0:
            h_near(p - 1).wait_recv()
            h_pass(p - 1).wait_recv()
    for dev in range(4):
        h_out(dev, 0, last, out_sem.at[2 + dev]).start()
    h_near(len(PARTS) - 1).wait_recv()
    h_pass(len(PARTS) - 1).wait_recv()
    for dev in range(4):
        h_out(dev, last, wide - last, out_sem.at[6 + dev]).start()
    for mask in (1, 2, 3):
        m_send(mask).wait_send()
    for c in range(steps):
        x_far(c).wait_send()
        x_near(c).wait_send()
        x_pass(c).wait_send()
    for kv in range(2):
        o_far(kv).wait_send()
        o_near(kv).wait_send()
        o_pass(kv).wait_send()
    for p in range(len(PARTS)):
        h_far(p).wait_send()
        h_near(p).wait_send()
        h_pass(p).wait_send()
    occ_out.wait()
    prep_out.wait()
    for dev in range(4):
        h_out(dev, 0, last, out_sem.at[2 + dev]).wait()
        h_out(dev, last, wide - last, out_sem.at[6 + dev]).wait()


def attend(x, ids_t, probs, w_q, w_k, w_v, w_o, group):
    tok, width = x.shape
    seq = tok * group
    kv_w = w_k.shape[1] // group
    kv_dev = kv_w // HEAD_DIM
    wide = w_q.shape[1] // group // kv_dev
    steps = width // wide
    dma = pltpu.SemaphoreType.DMA
    parts = len(PARTS)
    assert steps == 4 and kv_dev == 2 and group == 4
    return pl.pallas_call(
        attend_kernel,
        out_shape=(jax.ShapeDtypeStruct((seq, width), BF16), jax.ShapeDtypeStruct((1, OCC), jnp.int32),
                   jax.ShapeDtypeStruct((8, seq), F32)),
        in_specs=[ANY] * 7,
        out_specs=(ANY, ANY, ANY),
        scratch_shapes=[
            pltpu.VMEM((SLOTS * wide, wide), BF16),
            pltpu.VMEM((width, 2 * kv_w), BF16),
            pltpu.VMEM((seq, width), BF16),
            pltpu.VMEM((2, seq, group * wide), BF16),
            pltpu.VMEM((seq, HEAD_DIM), F32),
            pltpu.VMEM((seq, width), BF16),
            pltpu.VMEM((seq, wide), F32),
            pltpu.VMEM((seq, 2 * kv_w), F32),
            pltpu.VMEM((seq, wide), BF16),
            pltpu.VMEM((seq, 2 * kv_w), BF16),
            pltpu.VMEM(x.shape, BF16), pltpu.VMEM(ids_t.shape, jnp.int32), pltpu.VMEM(probs.shape, F32),
            pltpu.VMEM((1, OCC), jnp.int32), pltpu.VMEM((8, seq), F32),
            dma((SLOTS,)), dma((2, steps)), dma((parts, 4)), dma((3,)), dma((10,)),
        ] + [dma((steps,))] * 6 + [dma((2,))] * 6 + [dma((parts,))] * 6 + [dma((4,))] * 2,
        compiler_params=pltpu.CompilerParams(
            collective_id=0, has_side_effects=True, vmem_limit_bytes=66_000_000),
        cost_estimate=pl.CostEstimate(flops=seq * 2 * width * wide * 4, bytes_accessed=82_000_000, transcendentals=0),
        name='attend',
    )(x, ids_t, probs, w_q, w_k, w_v, w_o)


def dispatch_kernel(occ_hbm, prep_hbm, h_hbm, buf_hbm, out_hbm, occ_ref, h, prep_ref, zero, stage, todo, z_sem, s_sem, io_sem):
    me = lax.axis_index('sp')
    experts = buf_hbm.shape[0]
    tok = out_hbm.shape[0]
    h_copy = pltpu.make_async_copy(h_hbm, h, io_sem.at[0])
    prep_copy = pltpu.make_async_copy(prep_hbm, prep_ref, io_sem.at[1])
    out_copy = pltpu.make_async_copy(h.at[span(me * tok, tok)], out_hbm, io_sem.at[2])
    occ_copy = pltpu.make_async_copy(occ_hbm, occ_ref, io_sem.at[3])
    occ_copy.start()
    h_copy.start()
    prep_copy.start()
    zero[...] = jnp.zeros_like(zero)

    def fill(b):
        return pltpu.make_async_copy(zero.at[pl.ds(0, tok)], buf_hbm.at[b // 4, span(lax.rem(b, 4) * tok, tok)], z_sem.at[b])

    def fill_all(e):
        return pltpu.make_async_copy(zero, buf_hbm.at[e], z_sem.at[e * 4])

    def busy(e):
        return occ_ref[0, e * 4] + occ_ref[0, e * 4 + 1] + occ_ref[0, e * 4 + 2] + occ_ref[0, e * 4 + 3]

    def listed(b, count):
        one = occ_ref[0, b]

        @pl.when(one != 0)
        def _():
            todo[count] = b
        return count + one

    def first(e, count):
        used = busy(e)

        @pl.when(used == 0)
        def _():
            fill_all(e).start()

        @pl.when(used != 0)
        def _():
            at = count
            for i in range(4):
                b = e * 4 + i
                one = occ_ref[0, b]

                @pl.when(one == 0)
                def _():
                    fill(b).start()

                @pl.when(one != 0)
                def _():
                    todo[at] = b
                at = at + one
        return count + used

    for e in range(EARLY):
        fill_all(e).start()
    occ_copy.wait()
    count = lax.fori_loop(0, EARLY * 4, listed, 0)
    count = lax.fori_loop(EARLY, experts, first, count)
    batches = (count + BLOCKS - 1) // BLOCKS

    def put(batch, i):
        slot = lax.rem(batch, 2)
        b = todo[batch * BLOCKS + i]
        return pltpu.make_async_copy(stage.at[slot, pl.ds(i * tok, tok)],
                                     buf_hbm.at[b // 4, span(lax.rem(b, 4) * tok, tok)], s_sem.at[slot, i])

    def drain(batch):
        for i in range(BLOCKS):
            @pl.when(batch * BLOCKS + i < count)
            def _():
                put(batch, i).wait()

    row = lax.broadcasted_iota(jnp.int32, (BLOCKS * tok, 1), 0)
    prep_copy.wait()
    h_copy.wait()
    out_copy.start()
    for e in range(EARLY):
        fill_all(e).wait()

    def batch_step(batch, carry):
        @pl.when(batch >= 2)
        def _():
            drain(batch - 2)

        key = jnp.zeros((BLOCKS * tok, 1), jnp.int32)
        for i in range(BLOCKS):
            key = jnp.where(row // tok == i, todo[batch * BLOCKS + i], key)
        key = ((key + me * experts * 4) * tok + lax.rem(row, tok)).astype(F32)
        hit0 = key == prep_ref[0:1, :]
        hit1 = key == prep_ref[1:2, :]
        gate = jnp.sum(jnp.where(hit0, prep_ref[2:3, :], 0.0) + jnp.where(hit1, prep_ref[3:4, :], 0.0),
                       axis=1, keepdims=True)
        pick = jnp.where(hit0 | hit1, 1.0, 0.0).astype(BF16)
        stage[lax.rem(batch, 2)] = (gate * dot(pick, h[...])).astype(BF16)
        for i in range(BLOCKS):
            @pl.when(batch * BLOCKS + i < count)
            def _():
                put(batch, i).start()
        return carry

    lax.fori_loop(0, batches, batch_step, 0)

    @pl.when(batches >= 2)
    def _():
        drain(batches - 2)

    @pl.when(batches >= 1)
    def _():
        drain(batches - 1)

    def last(e, c):
        used = busy(e)

        @pl.when(used == 0)
        def _():
            fill_all(e).wait()

        @pl.when(used != 0)
        def _():
            for i in range(4):
                @pl.when(occ_ref[0, e * 4 + i] == 0)
                def _():
                    fill(e * 4 + i).wait()
        return c

    lax.fori_loop(EARLY, experts, last, 0)
    out_copy.wait()


def dispatch(occ, prep, h, experts, tok):
    seq, width = h.shape
    dma = pltpu.SemaphoreType.DMA
    return pl.pallas_call(
        dispatch_kernel,
        out_shape=(jax.ShapeDtypeStruct((experts, seq, width), BF16), jax.ShapeDtypeStruct((tok, width), BF16)),
        in_specs=[ANY, ANY, ANY],
        out_specs=(ANY, ANY),
        scratch_shapes=[pltpu.SMEM((1, OCC), jnp.int32), pltpu.VMEM((seq, width), BF16), pltpu.VMEM((8, seq), F32), pltpu.VMEM((seq, width), BF16),
                        pltpu.VMEM((2, BLOCKS * tok, width), BF16), pltpu.SMEM((experts * 4 + BLOCKS,), jnp.int32),
                        dma((experts * 4,)), dma((2, BLOCKS)), dma((4,))],
        compiler_params=pltpu.CompilerParams(vmem_limit_bytes=66_000_000),
        cost_estimate=pl.CostEstimate(flops=8_000_000_000, bytes_accessed=experts * seq * width * 2, transcendentals=0),
        name='dispatch',
    )(occ, prep, h)


def solution(mesh):
    group = mesh.shape['sp']
    row_spec = P(('dp', 'sp'), None)
    buf_spec = P(('dp', 'sp'), None, None)

    def device_step(x_loc, w_q, w_k, w_v, w_o, ids_loc, probs_loc):
        h, occ, prep = attend(x_loc, ids_loc.T, probs_loc, w_q, w_k, w_v, w_o, group)
        buf, hidden_out = dispatch(occ, prep, h, probs_loc.shape[1] // group, x_loc.shape[0])
        return hidden_out, buf

    return jax.shard_map(device_step, mesh=mesh, in_specs=(row_spec, P(), P(), P(), P(), row_spec, row_spec), out_specs=(row_spec, buf_spec), check_vma=False)
```

time: 550 us -> 48.6 us (0.09)
  blocking collectives: 357 us -> 0 us
  matrix products: 111 us -> 0 us
  local copies, waits for them, and re-layouts: 49.2 us -> 0 us
  Pallas kernels: 0 us -> 47.8 us
  waiting for transfers between devices: 15.7 us -> 0 us
  starting transfers between devices: 15 us -> 0 us
    all_to_all x1 -> x0, blocking collectives: 357 us -> none  [device_step(): recv_buf = lax.all_to_all(send_buf, 'sp', 0, 1, tiled=True)]
    dot_general x6 -> x0, matrix products: 110 us -> none  [the longest x1 48.7 us: device_step(): out_proj = jnp.dot(attn_loc, w_o, preferred_element_type=jnp.float32)]
    pallas_call x0 -> x2, Pallas kernels: none -> 47.8 us  [the longest x1 34.8 us: attend(): pl.pallas_call(attend_kernel, out_shape=(jax.ShapeDtypeStruct((seq, width...]
    all_to_all x5 -> x0, local copies, waits for them, and re-layouts: 21.5 us -> none  [the longest x1 21.4 us: device_step(): recv_buf = lax.all_to_all(send_buf, 'sp', 0, 1, tiled=True)]
    all_to_all x4 -> x0, waiting for transfers between devices: 15.7 us -> none  [the longest x1 7.03 us: device_step(): q_seq = lax.all_to_all(q_loc, 'sp', 1, 0, tiled=True)]
    all_to_all x4 -> x0, starting transfers between devices: 15 us -> none  [the longest x1 4.61 us: device_step(): k_seq = lax.all_to_all(k_loc, 'sp', 1, 0, tiled=True)]
    scatter x1 -> x0, local copies, waits for them, and re-layouts: 11.6 us -> none  [route_rows(): return send_buf.at[expert_ids, slot_rank].set(gated, unique_indices=True)]
    broadcast_in_dim x1 -> x0, local copies, waits for them, and re-layouts: 10.5 us -> none  [route_rows(): send_buf = jnp.zeros((experts, tok_dev, width), jnp.bfloat16)]
  transfers between devices with their start and end apart: 4 -> 0, of which waited for: 3 -> 0; matrix products, arithmetic and copies ran while one was open for 11% -> 0% of each run, Pallas kernels for 0% -> 0%
where the time goes in v2:
time: 48.6 us; the launch traced here: 48.5 us
  Pallas kernels  47.8 us (98%)
  between operations  0.64 us (1%)
    pallas_call x1, Pallas kernels, attend(): pl.pallas_call(attend_kernel, out_shape=(jax.ShapeDtypeStruct((seq, width...  34.8 us
    pallas_call x1, Pallas kernels, dispatch(): pl.pallas_call(dispatch_kernel, out_shape=(jax.ShapeDtypeStruct((experts,...  13 us

profile of v2, /device:TPU:0, one launch (start us, length us, event | category | flops | bytes accessed | tf_op | source)
XLA Modules:
  0.0 48.5 jit_solution(10779828998819607669)
XLA Ops:
  0.6 34.8 %attend.1 = (bf16[64,6144]{1,0:T(8,128)(2,1)}, s32[1,256]{1,0:T(1,128)}, f32[8,64]{1,0:T(8,128)}) custom-call(bf16[16,6144]{1,0:T(8,128)(2,1)} %x_hbm.1, s32[2,16]{1,0:T(2,128)} %bitcast.1, f32[16,160]{1,0:T(8,128)} %probs_hbm.1, bf16[6144,12288]{1,0:T(8,128)(2,1)} %wq_hbm.1, bf16[6144,1024]{1,0:T(8,128)(2,1)} %wk_hbm.1, bf16[6144,1024]{1,0:T(8,128)(2,1)} %wv_hbm.1, ...), custom_call_target="tpu_custom_call" | custom-call | flops 4831838208 | bytes 82000000 | tf_op jit(solution)/shard_map/attend/pallas_call | solution.py:350
  35.5 13.0 %dispatch.1 = (bf16[40,64,6144]{2,1,0:T(8,128)(2,1)}, bf16[16,6144]{1,0:T(8,128)(2,1)}) custom-call(s32[1,256]{1,0:T(1,128)} %get-tuple-element.7.occ_hbm, f32[8,64]{1,0:T(8,128)} %get-tuple-element.8.prep_hbm, bf16[64,6144]{1,0:T(8,128)(2,1)} %get-tuple-element.9.h_hbm), custom_call_target="tpu_custom_call" | custom-call | flops 8000000000 | bytes 31457280 | tf_op jit(solution)/shard_map/dispatch/pallas_call | solution.py:511

commit v3 on v2

v3 whole, which is shorter than its diff:
```python
import math
import jax
import jax.numpy as jnp
from jax import lax
from jax.experimental import pallas as pl
from jax.experimental.pallas import tpu as pltpu
from jax.sharding import PartitionSpec as P

HEAD_DIM = 128
SCORE_SCALE = 1.0 / math.sqrt(HEAD_DIM)
SLOTS = 10
PARTS = ((0, 1024), (1024, 256), (1280, 256))
SEGS = ((0, 1536), (0, 1024), (1024, 512))
EARLY = 4
PLACE = (8, 9, 0, 1, 2, 3, 4, 5)
MESH = pl.DeviceIdType.MESH
ANY = pl.BlockSpec(memory_space=pl.ANY)
VMEM = pl.BlockSpec(memory_space=pltpu.VMEM)
SMEM = pl.BlockSpec(memory_space=pltpu.SMEM)
F32, BF16 = jnp.float32, jnp.bfloat16


def peer_of(me, mask):
    chip = lax.rem(me // 2 + mask // 2, 2)
    core = lax.rem(lax.rem(me, 2) + mask % 2, 2)
    return chip * 2 + core


def span(start, size):
    return pl.ds(pl.multiple_of(start, size), size)


def dot(a, b):
    return jnp.dot(a, b, preferred_element_type=F32)


def attend_kernel(x_hbm, ids_hbm, probs_hbm, wq_hbm, wk_hbm, wv_hbm, wo_hbm, h_hbm, occ_hbm, prep_hbm,
                  ring, kv_buf, x_all, o_all, m_all, h_all, acc, kv_acc, q_ref, kv_ref, x_ref, ids_ref, probs_ref,
                  occ_ref, prep_ref, w_sem, kv_sem, p_sem, in_sem, out_sem, xs_snd, xs_rcv, xd_snd, xd_rcv, xf_snd, xf_rcv,
                  os_snd, os_rcv, od_snd, od_rcv, of_snd, of_rcv, hs_snd, hs_rcv, hd_snd, hd_rcv, hf_snd, hf_rcv, hg_snd,
                  m_snd, m_rcv):
    me = lax.axis_index('sp')
    tok, width = x_ref.shape
    seq = x_all.shape[0]
    wide = ring.shape[1]
    steps = width // wide
    kv_w = kv_buf.shape[1] // 2
    heads = wide // HEAD_DIM
    experts = probs_ref.shape[1] // 4
    core_mate = peer_of(me, 1)
    chip_mate = peer_of(me, 2)
    mine = span(me * tok, tok)
    theirs = span(chip_mate * tok, tok)

    def q_copy(c):
        rows = span(c * wide, wide)
        return pltpu.make_async_copy(wq_hbm.at[rows, span(me * 2 * wide, wide)], ring.at[rows], w_sem.at[c])

    def r_copy(seg, c):
        off, size = SEGS[seg]
        cols = pl.ds(pl.multiple_of((me * 2 + 1) * wide + off, 512), size)
        return pltpu.make_async_copy(wq_hbm.at[span(c * wide, wide), cols],
                                     ring.at[span((c + 4) * wide, wide), pl.ds(off, size)], w_sem.at[2 + 2 * seg + c // 2])

    def r_dot(seg, half):
        off, size = SEGS[seg]
        deep = 2 * wide
        base = 4 * wide + half * deep
        pltpu.make_async_copy(wq_hbm.at[pl.ds(0, deep), pl.ds(0, size)], ring.at[pl.ds(base, deep), pl.ds(off, size)],
                              w_sem.at[2 + 2 * seg + half]).wait()
        return dot(x_all[:, half * deep:(half + 1) * deep], ring[base:base + deep, off:off + size])

    def k_copy(c):
        rows = span(c * wide, wide)
        return pltpu.make_async_copy(wk_hbm.at[rows, span(me * kv_w, kv_w)], kv_buf.at[rows, pl.ds(0, kv_w)], kv_sem.at[c])

    def v_copy(c):
        rows = span(c * wide, wide)
        return pltpu.make_async_copy(wv_hbm.at[rows, span(me * kv_w, kv_w)], kv_buf.at[rows, pl.ds(kv_w, kv_w)], kv_sem.at[c])

    def p_sem_at(p, i):
        return i // 2 if p == 0 else 3 * p + 1 + (i + 2) // 4

    def p_copy(p, i):
        off, size = PARTS[p]
        return pltpu.make_async_copy(
            wo_hbm.at[span((peer_of(me, i % 4) * 2 + i // 4) * wide, wide), pl.ds(pl.multiple_of(me * wide + off, 128), size)],
            ring.at[pl.ds(PLACE[i] * wide, wide), pl.ds(off, size)], p_sem.at[p_sem_at(p, i)])

    def p_dot(p, i, count):
        off, size = PARTS[p]
        tile = ring.at[pl.ds(PLACE[i] * wide, count * wide), pl.ds(off, size)]
        pltpu.make_async_copy(wo_hbm.at[pl.ds(0, count * wide), pl.ds(0, size)], tile, p_sem.at[p_sem_at(p, i)]).wait()
        base = PLACE[i] * wide
        part = dot(o_all[:, i * wide:(i + count) * wide], ring[base:base + count * wide, off:off + size])
        if i == 0:
            acc[:, off:off + size] = part
        else:
            acc[:, off:off + size] += part

    def remote(src, dst, snd, rcv, to):
        return pltpu.make_async_remote_copy(src_ref=src, dst_ref=dst, send_sem=snd, recv_sem=rcv,
                                            device_id={'sp': to}, device_id_type=MESH)

    def x_far(c):
        cols = pl.ds(c * wide, wide)
        return remote(x_ref.at[:, cols], x_all.at[mine, cols], xs_snd, xs_rcv.at[c], chip_mate)

    def x_near(c):
        cols = pl.ds(c * wide, wide)
        return remote(x_ref.at[:, cols], x_all.at[mine, cols], xd_snd, xd_rcv.at[c], core_mate)

    def x_pass(c):
        cols = pl.ds(c * wide, wide)
        return remote(x_all.at[theirs, cols], x_all.at[theirs, cols], xf_snd, xf_rcv.at[c], core_mate)

    def o_part(seg, r):
        off, size = SEGS[seg]
        return o_all.at[:, pl.ds((min(seg, 1) * 4 + r) * wide + off, size)]

    def o_far(seg):
        return remote(o_part(seg, 0), o_part(seg, 2), os_snd, os_rcv.at[seg], chip_mate)

    def o_near(seg):
        return remote(o_part(seg, 0), o_part(seg, 1), od_snd, od_rcv.at[seg], core_mate)

    def o_pass(seg):
        return remote(o_part(seg, 2), o_part(seg, 3), of_snd, of_rcv.at[seg], core_mate)

    def h_part(p, dev):
        off, size = PARTS[p]
        return h_all.at[:, pl.ds(pl.multiple_of(dev * wide + off, 128), size)]

    def h_far(p):
        return remote(h_part(p, me), h_part(p, me), hs_snd, hs_rcv.at[p], chip_mate)

    def h_near(p):
        return remote(h_part(p, me), h_part(p, me), hd_snd, hd_rcv.at[p], core_mate)

    def h_pass(p):
        return remote(h_part(p, chip_mate), h_part(p, chip_mate), hf_snd, hf_rcv.at[p], core_mate)

    def h_diag():
        p = len(PARTS) - 1
        return remote(h_part(p, me), h_part(p, me), hg_snd, hf_rcv.at[p], peer_of(me, 3))

    def m_send(mask):
        return remote(m_all.at[mine], m_all.at[mine], m_snd, m_rcv.at[mask - 1], peer_of(me, mask))

    barrier = pltpu.get_barrier_semaphore()
    for mask in (1, 2, 3):
        pl.semaphore_signal(barrier, inc=1, device_id={'sp': peer_of(me, mask)}, device_id_type=MESH)
    x_in = pltpu.make_async_copy(x_hbm, x_ref, in_sem.at[0])
    ids_in = pltpu.make_async_copy(ids_hbm, ids_ref, in_sem.at[1])
    probs_in = pltpu.make_async_copy(probs_hbm, probs_ref, in_sem.at[2])
    x_in.start()
    ids_in.start()
    probs_in.start()

    def start_first(c, carry):
        q_copy(c).start()
        k_copy(c).start()
        v_copy(c).start()
        return carry

    def start_second(c, carry):
        r_copy(1, c).start()
        return carry

    def start_third(c, carry):
        r_copy(2, c).start()
        return carry

    lax.fori_loop(0, 4, start_first, 0)
    lax.fori_loop(0, 4, start_second, 0)
    lax.fori_loop(0, 4, start_third, 0)
    p_copy(0, 0).start()
    p_copy(0, 1).start()
    x_in.wait()
    pl.semaphore_wait(barrier, 3)
    for c in range(steps):
        x_far(c).start()
        x_near(c).start()
    x_all[mine, :] = x_ref[...]
    ids_in.wait()
    probs_in.wait()
    ids = ids_ref[...].astype(F32)
    probs = probs_ref[...]
    eye = lax.broadcasted_iota(jnp.int32, (tok, tok), 0) == lax.broadcasted_iota(jnp.int32, (tok, tok), 1)
    id0 = jnp.sum(jnp.where(eye, ids[0:1, :], 0.0), axis=1, keepdims=True)
    id1 = jnp.sum(jnp.where(eye, ids[1:2, :], 0.0), axis=1, keepdims=True)
    lanes = lax.broadcasted_iota(jnp.int32, probs.shape, 1).astype(F32)
    p0 = jnp.sum(jnp.where(lanes == id0, probs, 0.0), axis=1, keepdims=True)
    p1 = jnp.sum(jnp.where(lanes == id1, probs, 0.0), axis=1, keepdims=True)
    total = p0 + p1
    cols = lax.broadcasted_iota(jnp.int32, (tok, HEAD_DIM), 1)
    m_all[mine, :] = jnp.where(cols == 0, id0, jnp.where(cols == 1, id1,
                     jnp.where(cols == 2, p0 / total, jnp.where(cols == 3, p1 / total, 0.0))))
    for mask in (1, 2, 3):
        m_send(mask).start()
    def first_dots(c):
        x_near(c).wait_recv()
        x_pass(c).wait_recv()
        rows = pl.ds(c * wide, wide)
        pltpu.make_async_copy(wq_hbm.at[rows, pl.ds(0, 2 * kv_w)], kv_buf.at[rows, :], kv_sem.at[c]).wait()
        x = x_all[:, c * wide:(c + 1) * wide]
        part = dot(x, kv_buf[c * wide:(c + 1) * wide, :])
        if c == 0:
            kv_acc[...] = part
        else:
            kv_acc[...] += part
        q_copy(c).wait()
        part = dot(x, ring[c * wide:(c + 1) * wide, :])
        if c == 0:
            acc[...] = part
        else:
            acc[...] += part

    for c in range(steps):
        x_far(c).wait_recv()
        x_pass(c).start()
        if c > 0:
            first_dots(c - 1)
    first_dots(steps - 1)

    def attention(seg):
        kv = min(seg, 1)
        start, size = SEGS[seg]
        heads = size // HEAD_DIM
        k = kv_ref[:, kv * HEAD_DIM:(kv + 1) * HEAD_DIM]
        v = kv_ref[:, kv_w + kv * HEAD_DIM:kv_w + (kv + 1) * HEAD_DIM]
        cuts = [slice(start + m * HEAD_DIM, start + (m + 1) * HEAD_DIM) for m in range(heads)]
        q = jnp.concatenate([q_ref[:, c] for c in cuts], axis=0)
        s = lax.dot_general(q, k, (((1,), (1,)), ((), ())), preferred_element_type=F32) * SCORE_SCALE
        row = lax.rem(lax.broadcasted_iota(jnp.int32, s.shape, 0), seq)
        s = jnp.where(row >= lax.broadcasted_iota(jnp.int32, s.shape, 1), s, -1e30)
        e = jnp.exp(s - jnp.max(s, axis=1, keepdims=True))
        w = (e / jnp.sum(e, axis=1, keepdims=True)).astype(BF16)
        o = dot(w, v).astype(BF16)
        for m, c in enumerate(cuts):
            o_all[:, kv * 4 * wide + c.start:kv * 4 * wide + c.stop] = o[m * seq:(m + 1) * seq]
        o_far(seg).start()
        o_near(seg).start()

    kv_ref[...] = kv_acc[...].astype(BF16)
    q_ref[...] = acc[...].astype(BF16)
    for i in (2, 3, 4, 5):
        p_copy(0, i).start()
    attention(0)

    mid = SEGS[2][0]
    acc[:, :mid] = r_dot(1, 0)
    q_ref[:, :mid] = (acc[:, :mid] + r_dot(1, 1)).astype(BF16)
    attention(1)
    acc[:, mid:] = r_dot(2, 0)
    p_copy(0, 6).start()
    p_copy(0, 7).start()
    q_ref[:, mid:] = (acc[:, mid:] + r_dot(2, 1)).astype(BF16)
    for i in range(8):
        p_copy(1, i).start()
    attention(2)

    def routing():
        for mask in (1, 2, 3):
            m_send(mask).wait_recv()
        meta = m_all[...]
        rows = meta.T
        t_col = lax.broadcasted_iota(jnp.int32, (seq, seq), 0)
        t_row = lax.broadcasted_iota(jnp.int32, (seq, seq), 1)
        before = (t_col < t_row) & (t_col // tok == t_row // tok)
        source = (lax.broadcasted_iota(jnp.int32, (1, seq), 1) // tok).astype(F32)
        for k in range(2):
            same = (meta[:, 0:1] == rows[k:k + 1, :]) | (meta[:, 1:2] == rows[k:k + 1, :])
            rank = jnp.sum(jnp.where(before & same, 1.0, 0.0), axis=0, keepdims=True)
            prep_ref[k:k + 1, :] = (rows[k:k + 1, :] * 4.0 + source) * tok + rank
        prep_ref[2:4, :] = rows[2:4, :]
        prep_ref[4:8, :] = jnp.zeros((4, seq), F32)
        block = (lax.broadcasted_iota(jnp.int32, (seq, HEAD_DIM), 1) + me * experts).astype(F32)
        used = (meta[:, 0:1] == block) | (meta[:, 1:2] == block)
        occ_ref[...] = jnp.max(jnp.where(used, 1, 0), axis=0, keepdims=True)
        occ_out = pltpu.make_async_copy(occ_ref, occ_hbm, out_sem.at[0])
        prep_out = pltpu.make_async_copy(prep_ref, prep_hbm, out_sem.at[1])
        occ_out.start()
        prep_out.start()
        return occ_out, prep_out

    o_near(0).wait_recv()
    p_dot(0, 0, 2)
    for i in range(8):
        p_copy(2, i).start()
    occ_out, prep_out = routing()
    o_far(0).wait_recv()
    o_pass(0).start()
    o_far(1).wait_recv()
    o_pass(1).start()
    o_pass(0).wait_recv()
    p_dot(0, 2, 2)
    o_near(1).wait_recv()
    o_near(2).wait_recv()
    o_far(2).wait_recv()
    o_pass(2).start()
    p_dot(0, 4, 2)
    o_pass(1).wait_recv()
    o_pass(2).wait_recv()
    p_dot(0, 6, 2)
    for p, (off, size) in enumerate(PARTS):
        if p > 0:
            p_dot(p, 0, 2)
            p_dot(p, 2, 4)
            p_dot(p, 6, 2)
        home = pl.ds(pl.multiple_of(me * wide + off, 128), size)
        h_all[:, home] = (x_all[:, home].astype(F32) + acc[:, off:off + size]).astype(BF16)
        h_far(p).start()
        if p == len(PARTS) - 1:
            h_diag().start()
        h_near(p).start()

    last = PARTS[-1][0]

    def h_out(dev, off, size, sem):
        cut = pl.ds(dev * wide + off, size)
        return pltpu.make_async_copy(h_all.at[:, cut], h_hbm.at[:, cut], sem)

    for p in range(len(PARTS) - 1):
        h_far(p).wait_recv()
        h_pass(p).start()
    for p in range(len(PARTS) - 1):
        h_near(p).wait_recv()
        h_pass(p).wait_recv()
    for dev in range(4):
        h_out(dev, 0, last, out_sem.at[2]).start()
    h_near(len(PARTS) - 1).wait_recv()
    h_far(len(PARTS) - 1).wait_recv()
    h_diag().wait_recv()
    for dev in range(4):
        h_out(dev, last, wide - last, out_sem.at[3]).start()

    remote(m_all.at[pl.ds(0, 3 * tok)], m_all.at[pl.ds(0, 3 * tok)], m_snd, m_rcv.at[0], core_mate).wait_send()
    for snd in (xs_snd, xd_snd, xf_snd):
        remote(x_ref, x_all.at[mine], snd, xs_rcv.at[0], chip_mate).wait_send()
    both = o_all.at[:, pl.ds(0, 2 * wide)]
    for snd in (os_snd, od_snd, of_snd):
        remote(both, both, snd, os_rcv.at[0], chip_mate).wait_send()
    whole = h_all.at[:, pl.ds(0, wide)]
    for snd in (hs_snd, hd_snd):
        remote(whole, whole, snd, hs_rcv.at[0], chip_mate).wait_send()
    most = h_all.at[:, pl.ds(0, last)]
    remote(most, most, hf_snd, hf_rcv.at[0], core_mate).wait_send()
    h_diag().wait_send()
    occ_out.wait()
    prep_out.wait()
    for size, sem in ((last, 2), (wide - last, 3)):
        cut = pl.ds(0, 4 * size)
        pltpu.make_async_copy(h_all.at[:, cut], h_hbm.at[:, cut], out_sem.at[sem]).wait()


def attend(x, ids_t, probs, w_q, w_k, w_v, w_o, group):
    tok, width = x.shape
    seq = tok * group
    kv_w = w_k.shape[1] // group
    kv_dev = kv_w // HEAD_DIM
    wide = w_q.shape[1] // group // kv_dev
    steps = width // wide
    dma = pltpu.SemaphoreType.DMA
    parts = len(PARTS)
    assert steps == 4 and kv_dev == 2 and group == 4
    return pl.pallas_call(
        attend_kernel,
        out_shape=(jax.ShapeDtypeStruct((seq, width), BF16), jax.ShapeDtypeStruct((1, HEAD_DIM), jnp.int32),
                   jax.ShapeDtypeStruct((8, seq), F32)),
        in_specs=[ANY] * 7,
        out_specs=(ANY, ANY, ANY),
        scratch_shapes=[
            pltpu.VMEM((SLOTS * wide, wide), BF16),
            pltpu.VMEM((width, 2 * kv_w), BF16),
            pltpu.VMEM((seq, width), BF16),
            pltpu.VMEM((seq, 2 * group * wide), BF16),
            pltpu.VMEM((seq, HEAD_DIM), F32),
            pltpu.VMEM((seq, width), BF16),
            pltpu.VMEM((seq, wide), F32),
            pltpu.VMEM((seq, 2 * kv_w), F32),
            pltpu.VMEM((seq, wide), BF16),
            pltpu.VMEM((seq, 2 * kv_w), BF16),
            pltpu.VMEM(x.shape, BF16), pltpu.VMEM(ids_t.shape, jnp.int32), pltpu.VMEM(probs.shape, F32),
            pltpu.VMEM((1, HEAD_DIM), jnp.int32), pltpu.VMEM((8, seq), F32),
            dma((8,)), dma((steps,)), dma((3 * parts + 1,)), dma((3,)), dma((4,)),
        ] + [dma, dma((steps,))] * 3 + [dma, dma((3,))] * 3 + [dma, dma((parts,))] * 3 + [dma, dma, dma((3,))],
        compiler_params=pltpu.CompilerParams(
            collective_id=0, has_side_effects=True, vmem_limit_bytes=66_000_000),
        cost_estimate=pl.CostEstimate(flops=seq * 2 * width * wide * 4, bytes_accessed=82_000_000, transcendentals=0),
        name='attend',
    )(x, ids_t, probs, w_q, w_k, w_v, w_o)


def dispatch_kernel(occ_hbm, prep_hbm, h_hbm, buf_hbm, out_hbm, occ_ref, h, prep_ref, zero, stage, todo,
                    e_sem, z_sem, p_sem, io_sem):
    me = lax.axis_index('sp')
    experts, seq, _ = buf_hbm.shape
    tok = out_hbm.shape[0]
    occ_copy = pltpu.make_async_copy(occ_hbm, occ_ref, io_sem.at[0])
    h_copy = pltpu.make_async_copy(h_hbm, h, io_sem.at[1])
    prep_copy = pltpu.make_async_copy(prep_hbm, prep_ref, io_sem.at[2])
    out_copy = pltpu.make_async_copy(h.at[span(me * tok, tok)], out_hbm, io_sem.at[3])
    occ_copy.start()
    h_copy.start()
    prep_copy.start()
    zero[...] = jnp.zeros_like(zero)
    for e in range(EARLY):
        pltpu.make_async_copy(zero, buf_hbm.at[e], e_sem).start()
    occ_copy.wait()

    def listed(e, count):
        used = occ_ref[0, e]

        @pl.when(used != 0)
        def _():
            todo[count] = e
        return count + used

    def filled(e, count):
        @pl.when(occ_ref[0, e] == 0)
        def _():
            pltpu.make_async_copy(zero, buf_hbm.at[e], z_sem).start()
        return listed(e, count)

    count = lax.fori_loop(0, EARLY, listed, 0)
    count = lax.fori_loop(EARLY, experts, filled, count)
    prep_copy.wait()
    h_copy.wait()
    out_copy.start()
    pltpu.make_async_copy(stage.at[pl.ds(0, EARLY)], buf_hbm.at[pl.ds(0, EARLY)], e_sem).wait()
    row = lax.broadcasted_iota(jnp.int32, (2 * seq, 1), 0)

    def batch_step(batch, carry):
        at = batch * 2
        key = jnp.where(row < seq, todo[at], todo[at + 1])
        key = ((key + me * experts) * seq + lax.rem(row, seq)).astype(F32)
        hit0 = key == prep_ref[0:1, :]
        hit1 = key == prep_ref[1:2, :]
        gate = jnp.sum(jnp.where(hit0, prep_ref[2:3, :], 0.0) + jnp.where(hit1, prep_ref[3:4, :], 0.0),
                       axis=1, keepdims=True)
        pick = jnp.where(hit0 | hit1, 1.0, 0.0).astype(BF16)
        rows = (gate * dot(pick, h[...])).astype(BF16)
        for i in range(2):
            stage[at + i] = rows[i * seq:(i + 1) * seq]
        for i in range(2):
            e = todo[at + i]

            @pl.when((at + i < count) & (e < EARLY))
            def _():
                pltpu.make_async_copy(stage.at[at + i], buf_hbm.at[e], p_sem.at[e]).start()

            @pl.when((at + i < count) & (e >= EARLY))
            def _():
                pltpu.make_async_copy(stage.at[at + i], buf_hbm.at[e], z_sem).start()
        return carry

    lax.fori_loop(0, (count + 1) // 2, batch_step, 0)
    for e in range(EARLY):
        @pl.when(occ_ref[0, e] != 0)
        def _():
            pltpu.make_async_copy(zero, buf_hbm.at[e], p_sem.at[e]).wait()
    rest = pl.ds(EARLY, experts - EARLY)
    pltpu.make_async_copy(stage.at[rest], buf_hbm.at[rest], z_sem).wait()
    out_copy.wait()


def dispatch(occ, prep, h, experts, tok):
    seq, width = h.shape
    dma = pltpu.SemaphoreType.DMA
    return pl.pallas_call(
        dispatch_kernel,
        out_shape=(jax.ShapeDtypeStruct((experts, seq, width), BF16), jax.ShapeDtypeStruct((tok, width), BF16)),
        in_specs=[ANY, ANY, ANY],
        out_specs=(ANY, ANY),
        scratch_shapes=[pltpu.SMEM((1, HEAD_DIM), jnp.int32), pltpu.VMEM((seq, width), BF16), pltpu.VMEM((8, seq), F32),
                        pltpu.VMEM((seq, width), BF16), pltpu.VMEM((experts, seq, width), BF16),
                        pltpu.SMEM((experts + 2,), jnp.int32), dma, dma, dma((EARLY,)), dma((4,))],
        compiler_params=pltpu.CompilerParams(vmem_limit_bytes=66_000_000),
        cost_estimate=pl.CostEstimate(flops=8_000_000_000, bytes_accessed=experts * seq * width * 2, transcendentals=0),
        name='dispatch',
    )(occ, prep, h)


def solution(mesh):
    group = mesh.shape['sp']
    row_spec = P(('dp', 'sp'), None)
    buf_spec = P(('dp', 'sp'), None, None)

    def device_step(x_loc, w_q, w_k, w_v, w_o, ids_loc, probs_loc):
        h, occ, prep = attend(x_loc, ids_loc.T, probs_loc, w_q, w_k, w_v, w_o, group)
        buf, hidden_out = dispatch(occ, prep, h, probs_loc.shape[1] // group, x_loc.shape[0])
        return hidden_out, buf

    return jax.shard_map(device_step, mesh=mesh, in_specs=(row_spec, P(), P(), P(), P(), row_spec, row_spec), out_specs=(row_spec, buf_spec), check_vma=False)
```

time: 48.6 us -> 45.8 us (0.942)
  Pallas kernels: 47.8 us -> 45.5 us
    pallas_call x1, Pallas kernels: 13 us -> 11.1 us  [dispatch(): pl.pallas_call(dispatch_kernel, out_shape=(jax.ShapeDtypeStruct((experts,...]
    pallas_call x1, Pallas kernels: 34.8 us -> 34.3 us  [attend(): pl.pallas_call(attend_kernel, out_shape=(jax.ShapeDtypeStruct((seq, width...]
where the time goes in v3:
time: 45.8 us; the launch traced here: 46.1 us
  Pallas kernels  45.5 us (99%)
  between operations  0.64 us (1%)
    pallas_call x1, Pallas kernels, attend(): pl.pallas_call(attend_kernel, out_shape=(jax.ShapeDtypeStruct((seq, width...  34.3 us
    pallas_call x1, Pallas kernels, dispatch(): pl.pallas_call(dispatch_kernel, out_shape=(jax.ShapeDtypeStruct((experts,...  11.1 us

profile of v3, /device:TPU:0, one launch (start us, length us, event | category | flops | bytes accessed | tf_op | source)
XLA Modules:
  0.0 46.1 jit_solution(12915240734297427875)
XLA Ops:
  0.6 34.3 %attend.1 = (bf16[64,6144]{1,0:T(8,128)(2,1)}, s32[1,128]{1,0:T(1,128)}, f32[8,64]{1,0:T(8,128)}) custom-call(bf16[16,6144]{1,0:T(8,128)(2,1)} %x_hbm.1, s32[2,16]{1,0:T(2,128)} %bitcast.1, f32[16,160]{1,0:T(8,128)} %probs_hbm.1, bf16[6144,12288]{1,0:T(8,128)(2,1)} %wq_hbm.1, bf16[6144,1024]{1,0:T(8,128)(2,1)} %wk_hbm.1, bf16[6144,1024]{1,0:T(8,128)(2,1)} %wv_hbm.1, ...), custom_call_target="tpu_custom_call" | custom-call | flops 4831838208 | bytes 82000000 | tf_op jit(solution)/shard_map/attend/pallas_call | solution.py:367
  35.0 11.1 %dispatch.1 = (bf16[40,64,6144]{2,1,0:T(8,128)(2,1)}, bf16[16,6144]{1,0:T(8,128)(2,1)}) custom-call(s32[1,128]{1,0:T(1,128)} %get-tuple-element.7.occ_hbm, f32[8,64]{1,0:T(8,128)} %get-tuple-element.8.prep_hbm, bf16[64,6144]{1,0:T(8,128)(2,1)} %get-tuple-element.9.h_hbm), custom_call_target="tpu_custom_call" | custom-call | flops 8000000000 | bytes 31457280 | tf_op jit(solution)/shard_map/dispatch/pallas_call | solution.py:471

commit v4 on v3

v4 whole, which is shorter than its diff:
```python
import math
import jax
import jax.numpy as jnp
from jax import lax
from jax.experimental import pallas as pl
from jax.experimental.pallas import tpu as pltpu
from jax.sharding import PartitionSpec as P

HEAD_DIM = 128
SCORE_SCALE = 1.0 / math.sqrt(HEAD_DIM)
SLOTS = 10
PARTS = ((0, 512), (512, 512), (1024, 512))
HEAD = 512
SEGS = ((0, 1536), (0, 1024), (1024, 512))
EARLY = 4
ZERO_FIRST = 30
BLOCKS = 8
OCC = 256
PLACE = (8, 9, 0, 1, 2, 3, 4, 5)
MESH = pl.DeviceIdType.MESH
ANY = pl.BlockSpec(memory_space=pl.ANY)
VMEM = pl.BlockSpec(memory_space=pltpu.VMEM)
SMEM = pl.BlockSpec(memory_space=pltpu.SMEM)
F32, BF16 = jnp.float32, jnp.bfloat16


def peer_of(me, mask):
    chip = lax.rem(me // 2 + mask // 2, 2)
    core = lax.rem(lax.rem(me, 2) + mask % 2, 2)
    return chip * 2 + core


def span(start, size):
    return pl.ds(pl.multiple_of(start, size), size)


def dot(a, b):
    return jnp.dot(a, b, preferred_element_type=F32)


def attend_kernel(x_hbm, ids_hbm, probs_hbm, wq_hbm, wk_hbm, wv_hbm, wo_hbm, head_hbm, tail_hbm, occ_hbm, prep_hbm,
                  ring, kv_buf, x_all, o_all, m_all, h_all, acc, kv_acc, q_ref, kv_ref, x_ref, ids_ref, probs_ref,
                  occ_ref, prep_ref, w_sem, p_sem, in_sem, out_sem, x_snd, xs_rcv, xd_rcv, os_rcv, od_rcv, of_rcv,
                  hs_rcv, hd_rcv, hf_rcv, m_snd, m_rcv):
    me = lax.axis_index('sp')
    tok, width = x_ref.shape
    seq = x_all.shape[0]
    wide = ring.shape[1]
    steps = width // wide
    kv_w = kv_buf.shape[1] // 2
    heads = wide // HEAD_DIM
    experts = probs_ref.shape[1] // 4
    core_mate = peer_of(me, 1)
    chip_mate = peer_of(me, 2)
    mine = span(me * tok, tok)
    theirs = span(chip_mate * tok, tok)

    def q_copy(c):
        rows = span(c * wide, wide)
        return pltpu.make_async_copy(wq_hbm.at[rows, span(me * 2 * wide, wide)], ring.at[rows], w_sem.at[c])

    def r_copy(seg, c):
        off, size = SEGS[seg]
        cols = pl.ds(pl.multiple_of((me * 2 + 1) * wide + off, 512), size)
        return pltpu.make_async_copy(wq_hbm.at[span(c * wide, wide), cols],
                                     ring.at[span((c + 4) * wide, wide), pl.ds(off, size)], w_sem.at[2 + 2 * seg + c // 2])

    def r_dot(seg, half):
        off, size = SEGS[seg]
        deep = 2 * wide
        base = 4 * wide + half * deep
        pltpu.make_async_copy(wq_hbm.at[pl.ds(0, deep), pl.ds(0, size)], ring.at[pl.ds(base, deep), pl.ds(off, size)],
                              w_sem.at[2 + 2 * seg + half]).wait()
        return dot(x_all[:, half * deep:(half + 1) * deep], ring[base:base + deep, off:off + size])

    def k_copy(c):
        rows = span(c * wide, wide)
        return pltpu.make_async_copy(wk_hbm.at[rows, span(me * kv_w, kv_w)], kv_buf.at[rows, pl.ds(0, kv_w)], w_sem.at[c])

    def v_copy(c):
        rows = span(c * wide, wide)
        return pltpu.make_async_copy(wv_hbm.at[rows, span(me * kv_w, kv_w)], kv_buf.at[rows, pl.ds(kv_w, kv_w)], w_sem.at[c])

    def p_sem_at(p, i):
        return i // 2 if p == 0 else 4 + (i + 2) // 4 if p == 1 else 7 + (i + 2) // 4 + i // 7

    def p_copy(p, i):
        off, size = PARTS[p]
        return pltpu.make_async_copy(
            wo_hbm.at[span((peer_of(me, i % 4) * 2 + i // 4) * wide, wide), pl.ds(pl.multiple_of(me * wide + off, 128), size)],
            ring.at[pl.ds(PLACE[i] * wide, wide), pl.ds(off, size)], p_sem.at[p_sem_at(p, i)])

    def p_dot(p, i, count):
        off, size = PARTS[p]
        tile = ring.at[pl.ds(PLACE[i] * wide, count * wide), pl.ds(off, size)]
        pltpu.make_async_copy(wo_hbm.at[pl.ds(0, count * wide), pl.ds(0, size)], tile, p_sem.at[p_sem_at(p, i)]).wait()
        base = PLACE[i] * wide
        part = dot(o_all[:, i * wide:(i + count) * wide], ring[base:base + count * wide, off:off + size])
        if i == 0:
            acc[:, off:off + size] = part
        else:
            acc[:, off:off + size] += part

    def remote(src, dst, snd, rcv, to):
        return pltpu.make_async_remote_copy(src_ref=src, dst_ref=dst, send_sem=snd, recv_sem=rcv,
                                            device_id={'sp': to}, device_id_type=MESH)

    def x_far(c):
        cols = pl.ds(c * wide, wide)
        return remote(x_ref.at[:, cols], x_all.at[mine, cols], x_snd, xs_rcv.at[c], chip_mate)

    def x_near(c):
        cols = pl.ds(c * wide, wide)
        return remote(x_ref.at[:, cols], x_all.at[mine, cols], x_snd, xd_rcv.at[c], core_mate)

    def x_pass(c):
        cols = pl.ds(c * wide, wide)
        return remote(x_all.at[theirs, cols], x_all.at[theirs, cols], x_snd, xd_rcv.at[c], core_mate)

    def o_part(seg, r):
        off, size = SEGS[seg]
        return o_all.at[:, pl.ds((min(seg, 1) * 4 + r) * wide + off, size)]

    def o_far(seg):
        return remote(o_part(seg, 0), o_part(seg, 2), x_snd, os_rcv.at[seg], chip_mate)

    def o_near(seg):
        return remote(o_part(seg, 0), o_part(seg, 1), x_snd, od_rcv.at[seg], core_mate)

    def o_pass(seg):
        return remote(o_part(seg, 2), o_part(seg, 3), x_snd, of_rcv.at[seg], core_mate)

    def h_part(p, dev):
        off, size = PARTS[p]
        return h_all.at[:, pl.ds(pl.multiple_of(dev * wide + off, 128), size)]

    def h_far(p):
        return remote(h_part(p, me), h_part(p, me), x_snd, hs_rcv, chip_mate)

    def h_near(p):
        return remote(h_part(p, me), h_part(p, me), x_snd, hd_rcv, core_mate)

    def h_pass(p):
        return remote(h_part(p, chip_mate), h_part(p, chip_mate), x_snd, hf_rcv, core_mate)

    def m_send(mask):
        return remote(m_all.at[mine], m_all.at[mine], m_snd, m_rcv, peer_of(me, mask))

    barrier = pltpu.get_barrier_semaphore()
    for mask in (1, 2, 3):
        pl.semaphore_signal(barrier, inc=1, device_id={'sp': peer_of(me, mask)}, device_id_type=MESH)
    x_in = pltpu.make_async_copy(x_hbm, x_ref, in_sem.at[0])
    ids_in = pltpu.make_async_copy(ids_hbm, ids_ref, in_sem.at[1])
    probs_in = pltpu.make_async_copy(probs_hbm, probs_ref, in_sem.at[2])
    x_in.start()
    ids_in.start()
    probs_in.start()

    def start_first(c, carry):
        q_copy(c).start()
        k_copy(c).start()
        v_copy(c).start()
        return carry

    def start_second(c, carry):
        r_copy(1, c).start()
        return carry

    def start_third(c, carry):
        r_copy(2, c).start()
        return carry

    lax.fori_loop(0, 4, start_first, 0)
    lax.fori_loop(0, 4, start_second, 0)
    lax.fori_loop(0, 4, start_third, 0)
    p_copy(0, 0).start()
    p_copy(0, 1).start()
    x_in.wait()
    pl.semaphore_wait(barrier, 3)
    for c in range(steps):
        x_far(c).start()
        x_near(c).start()
    x_all[mine, :] = x_ref[...]
    ids_in.wait()
    probs_in.wait()
    ids = ids_ref[...].astype(F32)
    probs = probs_ref[...]
    eye = lax.broadcasted_iota(jnp.int32, (tok, tok), 0) == lax.broadcasted_iota(jnp.int32, (tok, tok), 1)
    id0 = jnp.sum(jnp.where(eye, ids[0:1, :], 0.0), axis=1, keepdims=True)
    id1 = jnp.sum(jnp.where(eye, ids[1:2, :], 0.0), axis=1, keepdims=True)
    lanes = lax.broadcasted_iota(jnp.int32, probs.shape, 1).astype(F32)
    p0 = jnp.sum(jnp.where(lanes == id0, probs, 0.0), axis=1, keepdims=True)
    p1 = jnp.sum(jnp.where(lanes == id1, probs, 0.0), axis=1, keepdims=True)
    total = p0 + p1
    cols = lax.broadcasted_iota(jnp.int32, (tok, HEAD_DIM), 1)
    m_all[mine, :] = jnp.where(cols == 0, id0, jnp.where(cols == 1, id1,
                     jnp.where(cols == 2, p0 / total, jnp.where(cols == 3, p1 / total, 0.0))))
    for mask in (1, 2, 3):
        m_send(mask).start()
    def first_dots(c):
        pair = x_all.at[pl.ds(0, 2 * tok), pl.ds(c * wide, wide)]
        remote(pair, pair, x_snd, xd_rcv.at[c], core_mate).wait_recv()
        chunk = pl.ds(0, wide + 2 * kv_w)
        pltpu.make_async_copy(wq_hbm.at[chunk, pl.ds(0, wide)], ring.at[chunk], w_sem.at[c]).wait()
        x = x_all[:, c * wide:(c + 1) * wide]
        part = dot(x, kv_buf[c * wide:(c + 1) * wide, :])
        if c == 0:
            kv_acc[...] = part
        else:
            kv_acc[...] += part
        part = dot(x, ring[c * wide:(c + 1) * wide, :])
        if c == 0:
            acc[...] = part
        else:
            acc[...] += part

    for c in range(steps):
        x_far(c).wait_recv()
        x_pass(c).start()
        if c > 0:
            first_dots(c - 1)
    first_dots(steps - 1)

    def attention(seg):
        kv = min(seg, 1)
        start, size = SEGS[seg]
        heads = size // HEAD_DIM
        k = kv_ref[:, kv * HEAD_DIM:(kv + 1) * HEAD_DIM]
        v = kv_ref[:, kv_w + kv * HEAD_DIM:kv_w + (kv + 1) * HEAD_DIM]
        cuts = [slice(start + m * HEAD_DIM, start + (m + 1) * HEAD_DIM) for m in range(heads)]
        q = jnp.concatenate([q_ref[:, c] for c in cuts], axis=0)
        s = lax.dot_general(q, k, (((1,), (1,)), ((), ())), preferred_element_type=F32) * SCORE_SCALE
        row = lax.rem(lax.broadcasted_iota(jnp.int32, s.shape, 0), seq)
        s = jnp.where(row >= lax.broadcasted_iota(jnp.int32, s.shape, 1), s, -1e30)
        e = jnp.exp(s - jnp.max(s, axis=1, keepdims=True))
        w = (e / jnp.sum(e, axis=1, keepdims=True)).astype(BF16)
        o = dot(w, v).astype(BF16)
        for m, c in enumerate(cuts):
            o_all[:, kv * 4 * wide + c.start:kv * 4 * wide + c.stop] = o[m * seq:(m + 1) * seq]
        o_far(seg).start()
        o_near(seg).start()

    kv_ref[...] = kv_acc[...].astype(BF16)
    q_ref[...] = acc[...].astype(BF16)
    for i in (2, 3, 4, 5):
        p_copy(0, i).start()
    attention(0)

    mid = SEGS[2][0]
    acc[:, :mid] = r_dot(1, 0)
    q_ref[:, :mid] = (acc[:, :mid] + r_dot(1, 1)).astype(BF16)
    attention(1)
    acc[:, mid:] = r_dot(2, 0)
    p_copy(0, 6).start()
    p_copy(0, 7).start()
    q_ref[:, mid:] = (acc[:, mid:] + r_dot(2, 1)).astype(BF16)
    for i in range(8):
        p_copy(1, i).start()
    attention(2)

    def routing():
        remote(m_all.at[pl.ds(0, 3 * tok)], m_all.at[pl.ds(0, 3 * tok)], m_snd, m_rcv, core_mate).wait_recv()
        meta = m_all[...]
        rows = meta.T
        t_col = lax.broadcasted_iota(jnp.int32, (seq, seq), 0)
        t_row = lax.broadcasted_iota(jnp.int32, (seq, seq), 1)
        before = (t_col < t_row) & (t_col // tok == t_row // tok)
        source = (lax.broadcasted_iota(jnp.int32, (1, seq), 1) // tok).astype(F32)
        for k in range(2):
            same = (meta[:, 0:1] == rows[k:k + 1, :]) | (meta[:, 1:2] == rows[k:k + 1, :])
            rank = jnp.sum(jnp.where(before & same, 1.0, 0.0), axis=0, keepdims=True)
            prep_ref[k:k + 1, :] = (rows[k:k + 1, :] * 4.0 + source) * tok + rank
        prep_ref[2:4, :] = rows[2:4, :]
        prep_ref[4:8, :] = jnp.zeros((4, seq), F32)
        block = (lax.broadcasted_iota(jnp.int32, (seq, OCC), 1) + me * experts * 4).astype(F32)
        origin = (lax.broadcasted_iota(jnp.int32, (seq, 1), 0) // tok).astype(F32)
        used = (meta[:, 0:1] * 4.0 + origin == block) | (meta[:, 1:2] * 4.0 + origin == block)
        occ_ref[...] = jnp.max(jnp.where(used, 1, 0), axis=0, keepdims=True)
        occ_out = pltpu.make_async_copy(occ_ref, occ_hbm, out_sem.at[0])
        prep_out = pltpu.make_async_copy(prep_ref, prep_hbm, out_sem.at[1])
        occ_out.start()
        prep_out.start()
        return occ_out, prep_out

    def finish(p):
        off, size = PARTS[p]
        home = pl.ds(pl.multiple_of(me * wide + off, 512), size)
        h_all[:, home] = (x_all[:, home].astype(F32) + acc[:, off:off + size]).astype(BF16)
        if p == 0:
            h_far(0).start()
        h_near(p).start()

    o_near(0).wait_recv()
    p_dot(0, 0, 2)
    for i in range(8):
        p_copy(2, i).start()
    occ_out, prep_out = routing()
    o_far(0).wait_recv()
    o_pass(0).start()
    o_near(1).wait_recv()
    o_near(2).wait_recv()
    p_dot(0, 4, 2)
    o_pass(0).wait_recv()
    p_dot(0, 2, 2)
    p_dot(1, 0, 2)
    o_far(1).wait_recv()
    o_pass(1).start()
    p_dot(1, 2, 4)
    o_far(2).wait_recv()
    o_pass(2).start()
    o_pass(1).wait_recv()
    o_pass(2).wait_recv()
    p_dot(0, 6, 2)
    finish(0)
    p_dot(1, 6, 2)
    finish(1)
    p_dot(2, 0, 2)
    p_dot(2, 2, 4)
    p_dot(2, 6, 1)
    p_dot(2, 7, 1)
    finish(2)

    h_far(0).wait_recv()
    h_pass(0).start()
    whole = h_all.at[:, pl.ds(0, wide)]
    remote(whole, whole, x_snd, hd_rcv, core_mate).wait_recv()
    for core in range(2):
        rest = wide - HEAD
        cut = pl.ds(pl.multiple_of((me // 2 * 2 + core) * wide + HEAD, 512), rest)
        pltpu.make_async_copy(h_all.at[:, cut], tail_hbm.at[:, pl.ds(core * rest, rest)], out_sem.at[3]).start()
    h_pass(0).wait_recv()
    for dev in range(4):
        pltpu.make_async_copy(h_all.at[:, pl.ds(dev * wide, HEAD)], head_hbm.at[:, pl.ds(dev * HEAD, HEAD)],
                              out_sem.at[2]).start()

    remote(m_all.at[pl.ds(0, 3 * tok)], m_all.at[pl.ds(0, 3 * tok)], m_snd, m_rcv, core_mate).wait_send()
    sent = (3 * tok * width + 6 * seq * wide + seq * wide + 2 * seq * HEAD) // 1024
    sends = ring.at[pl.ds(0, sent), pl.ds(0, 1024)]
    remote(sends, sends, x_snd, hs_rcv, core_mate).wait_send()
    occ_out.wait()
    prep_out.wait()
    pltpu.make_async_copy(h_all.at[:, pl.ds(0, 2 * (wide - HEAD))], tail_hbm, out_sem.at[3]).wait()
    pltpu.make_async_copy(h_all.at[:, pl.ds(0, 4 * HEAD)], head_hbm, out_sem.at[2]).wait()


def attend(x, ids_t, probs, w_q, w_k, w_v, w_o, group):
    tok, width = x.shape
    seq = tok * group
    kv_w = w_k.shape[1] // group
    kv_dev = kv_w // HEAD_DIM
    wide = w_q.shape[1] // group // kv_dev
    steps = width // wide
    dma = pltpu.SemaphoreType.DMA
    parts = len(PARTS)
    assert steps == 4 and kv_dev == 2 and group == 4
    return pl.pallas_call(
        attend_kernel,
        out_shape=(jax.ShapeDtypeStruct((seq, 4 * HEAD), BF16), jax.ShapeDtypeStruct((seq, 2 * (wide - HEAD)), BF16),
                   jax.ShapeDtypeStruct((1, OCC), jnp.int32),
                   jax.ShapeDtypeStruct((8, seq), F32)),
        in_specs=[ANY] * 7,
        out_specs=(ANY, ANY, ANY, ANY),
        scratch_shapes=[
            pltpu.VMEM((SLOTS * wide, wide), BF16),
            pltpu.VMEM((width, 2 * kv_w), BF16),
            pltpu.VMEM((seq, width), BF16),
            pltpu.VMEM((seq, 2 * group * wide), BF16),
            pltpu.VMEM((seq, HEAD_DIM), F32),
            pltpu.VMEM((seq, width), BF16),
            pltpu.VMEM((seq, wide), F32),
            pltpu.VMEM((seq, 2 * kv_w), F32),
            pltpu.VMEM((seq, wide), BF16),
            pltpu.VMEM((seq, 2 * kv_w), BF16),
            pltpu.VMEM(x.shape, BF16), pltpu.VMEM(ids_t.shape, jnp.int32), pltpu.VMEM(probs.shape, F32),
            pltpu.VMEM((1, OCC), jnp.int32), pltpu.VMEM((8, seq), F32),
            dma((8,)), dma((11,)), dma((3,)), dma((4,)),
            dma, dma((steps,)), dma((steps,)), dma((3,)), dma((3,)), dma((3,)), dma, dma, dma, dma, dma],
        compiler_params=pltpu.CompilerParams(
            collective_id=0, has_side_effects=True, vmem_limit_bytes=66_000_000),
        cost_estimate=pl.CostEstimate(flops=seq * 2 * width * wide * 4, bytes_accessed=82_000_000, transcendentals=0),
        name='attend',
    )(x, ids_t, probs, w_q, w_k, w_v, w_o)


def zero_kernel(occ_hbm, buf_hbm, list_hbm, occ_ref, list_ref, zero, z_sem, io_sem):
    experts = buf_hbm.shape[0]
    occ_copy = pltpu.make_async_copy(occ_hbm, occ_ref, io_sem.at[0])
    list_copy = pltpu.make_async_copy(list_ref, list_hbm, io_sem.at[1])
    occ_copy.start()
    zero[...] = jnp.zeros_like(zero)
    lax.fori_loop(0, ZERO_FIRST, lambda e, c: (pltpu.make_async_copy(zero, buf_hbm.at[e], z_sem).start(), c)[1], 0)
    occ_copy.wait()

    def expert(e, count):
        for i in range(4):
            one = occ_ref[0, e * 4 + i]

            @pl.when(one != 0)
            def _():
                list_ref[0, count] = e * 4 + i
            count = count + one
        return count

    list_ref[0, OCC - 1] = lax.fori_loop(0, experts, expert, 0)
    list_copy.start()
    filled = buf_hbm.at[pl.ds(0, ZERO_FIRST)]
    pltpu.make_async_copy(filled, filled, z_sem).wait()
    list_copy.wait()


def zero_most(occ, experts, seq, width):
    dma = pltpu.SemaphoreType.DMA
    return pl.pallas_call(
        zero_kernel,
        out_shape=(jax.ShapeDtypeStruct((experts, seq, width), BF16), jax.ShapeDtypeStruct((1, OCC), jnp.int32)),
        in_specs=[ANY],
        out_specs=(ANY, ANY),
        scratch_shapes=[pltpu.SMEM((1, OCC), jnp.int32), pltpu.SMEM((1, OCC), jnp.int32), pltpu.VMEM((seq, width), BF16),
                        dma, dma((2,))],
        compiler_params=pltpu.CompilerParams(vmem_limit_bytes=67_043_328),
        cost_estimate=pl.CostEstimate(flops=8_000_000_000, bytes_accessed=ZERO_FIRST * seq * width * 2, transcendentals=0),
        name='zero_most',
    )(occ)


def dispatch_kernel(list_hbm, occ_hbm, prep_hbm, head_hbm, tail_hbm, far_hbm, buf_in, buf_hbm, out_hbm, list_ref, occ_ref,
                    h, prep_ref, zero, stage, e_sem, z_sem, p_sem, io_sem, h_sem):
    me = lax.axis_index('sp')
    experts, seq, width = buf_hbm.shape
    tok = out_hbm.shape[0]
    wide = width // 4
    rest = wide - HEAD
    settled = ZERO_FIRST + EARLY
    list_copy = pltpu.make_async_copy(list_hbm, list_ref, io_sem.at[0])
    occ_copy = pltpu.make_async_copy(occ_hbm, occ_ref, io_sem.at[1])
    prep_copy = pltpu.make_async_copy(prep_hbm, prep_ref, io_sem.at[2])
    out_copy = pltpu.make_async_copy(h.at[span(me * tok, tok)], out_hbm, io_sem.at[3])
    list_copy.start()
    occ_copy.start()
    prep_copy.start()
    for dev in range(4):
        pltpu.make_async_copy(head_hbm.at[:, pl.ds(dev * HEAD, HEAD)], h.at[:, pl.ds(dev * wide, HEAD)], h_sem).start()
    for chip, src in ((me // 2, tail_hbm), (1 - me // 2, far_hbm)):
        for core in range(2):
            cut = pl.ds(pl.multiple_of((chip * 2 + core) * wide + HEAD, 512), rest)
            pltpu.make_async_copy(src.at[:, pl.ds(core * rest, rest)], h.at[:, cut], h_sem).start()
    zero[...] = jnp.zeros_like(zero)
    for e in range(ZERO_FIRST, settled):
        pltpu.make_async_copy(zero, buf_hbm.at[e], e_sem).start()
    list_copy.wait()
    occ_copy.wait()

    def place(b):
        return buf_hbm.at[b // 4, span(lax.rem(b, 4) * tok, tok)]

    def fill(e, carry):
        ones = [occ_ref[0, e * 4 + i] for i in range(4)]
        used = ones[0] + ones[1] + ones[2] + ones[3]

        @pl.when(used == 0)
        def _():
            pltpu.make_async_copy(zero, buf_hbm.at[e], z_sem).start()

        @pl.when(used != 0)
        def _():
            for i in range(4):
                @pl.when(ones[i] == 0)
                def _():
                    pltpu.make_async_copy(zero.at[pl.ds(0, tok)], place(e * 4 + i), z_sem).start()
        return carry

    lax.fori_loop(settled, experts, fill, 0)
    count = list_ref[0, OCC - 1]
    prep_copy.wait()
    pltpu.make_async_copy(buf_hbm.at[0], h, h_sem).wait()
    out_copy.start()
    row = lax.broadcasted_iota(jnp.int32, (BLOCKS * tok, 1), 0)

    def batch_step(batch, carry):
        at = batch * BLOCKS
        key = jnp.zeros((BLOCKS * tok, 1), jnp.int32)
        for i in range(BLOCKS):
            key = jnp.where(row // tok == i, list_ref[0, at + i], key)
        key = ((key + me * experts * 4) * tok + lax.rem(row, tok)).astype(F32)
        hit0 = key == prep_ref[0:1, :]
        hit1 = key == prep_ref[1:2, :]
        gate = jnp.sum(jnp.where(hit0, prep_ref[2:3, :], 0.0) + jnp.where(hit1, prep_ref[3:4, :], 0.0),
                       axis=1, keepdims=True)
        pick = jnp.where(hit0 | hit1, 1.0, 0.0).astype(BF16)
        rows = (gate * dot(pick, h[...])).astype(BF16)
        for i in range(BLOCKS):
            stage[at + i] = rows[i * tok:(i + 1) * tok]

        @pl.when(batch == 0)
        def _():
            early = buf_hbm.at[pl.ds(ZERO_FIRST, EARLY)]
            pltpu.make_async_copy(early, early, e_sem).wait()

        for i in range(BLOCKS):
            b = list_ref[0, at + i]

            @pl.when((at + i < count) & (b < settled * 4))
            def _():
                pltpu.make_async_copy(stage.at[at + i], place(b), p_sem).start()

            @pl.when((at + i < count) & (b >= settled * 4))
            def _():
                pltpu.make_async_copy(stage.at[at + i], place(b), z_sem).start()
        return carry

    lax.fori_loop(0, jnp.maximum((count + BLOCKS - 1) // BLOCKS, 1), batch_step, 0)

    def landed(i, carry):
        @pl.when(list_ref[0, i] < settled * 4)
        def _():
            pltpu.make_async_copy(stage.at[0], place(0), p_sem).wait()
        return carry

    lax.fori_loop(0, count, landed, 0)
    others = buf_hbm.at[pl.ds(settled, experts - settled)]
    pltpu.make_async_copy(others, others, z_sem).wait()
    out_copy.wait()


def dispatch(blocks, occ, prep, head, tail, far, buf, tok):
    experts, seq, width = buf.shape
    dma = pltpu.SemaphoreType.DMA
    return pl.pallas_call(
        dispatch_kernel,
        out_shape=(jax.ShapeDtypeStruct(buf.shape, BF16), jax.ShapeDtypeStruct((tok, width), BF16)),
        in_specs=[ANY] * 7,
        out_specs=(ANY, ANY),
        input_output_aliases={6: 0},
        scratch_shapes=[pltpu.SMEM((1, OCC), jnp.int32), pltpu.SMEM((1, OCC), jnp.int32),
                        pltpu.VMEM((seq, width), BF16), pltpu.VMEM((8, seq), F32), pltpu.VMEM((seq, width), BF16),
                        pltpu.VMEM((experts * 4, tok, width), BF16), dma, dma, dma, dma((4,)), dma],
        compiler_params=pltpu.CompilerParams(vmem_limit_bytes=66_000_000),
        cost_estimate=pl.CostEstimate(flops=4_000_000_000, bytes_accessed=experts * seq * width, transcendentals=0),
        name='dispatch',
    )(blocks, occ, prep, head, tail, far, buf)


def solution(mesh):
    group = mesh.shape['sp']
    row_spec = P(('dp', 'sp'), None)
    buf_spec = P(('dp', 'sp'), None, None)

    def device_step(x_loc, w_q, w_k, w_v, w_o, ids_loc, probs_loc):
        head, tail, occ, prep = attend(x_loc, ids_loc.T, probs_loc, w_q, w_k, w_v, w_o, group)
        far = lax.ppermute(tail, 'sp', [(i, (i + 2) % group) for i in range(group)])
        buf, blocks = zero_most(occ, probs_loc.shape[1] // group, head.shape[0], x_loc.shape[1])
        buf, hidden_out = dispatch(blocks, occ, prep, head, tail, far, buf, x_loc.shape[0])
        return hidden_out, buf

    return jax.shard_map(device_step, mesh=mesh, in_specs=(row_spec, P(), P(), P(), P(), row_spec, row_spec), out_specs=(row_spec, buf_spec), check_vma=False)
```

time: 45.8 us -> 44.6 us (0.974); the launches traced: 46.1 us -> 44.2 us
  Pallas kernels: 45.5 us -> 42.8 us
  starting transfers between devices: 0 us -> 0.74 us
    pallas_call x2 -> x3, Pallas kernels: 45.5 us -> 42.8 us  [the longest x1 31.2 us: attend(): pl.pallas_call(attend_kernel, out_shape=(jax.ShapeDtypeStruct((seq, 4 * H...]
    ppermute x0 -> x1, starting transfers between devices: none -> 0.74 us  [device_step(): far = lax.ppermute(tail, 'sp', [(i, (i + 2) % group) for i in range(group)])]
  transfers between devices with their start and end apart: 0 -> 1, of which waited for: 0 -> 0; matrix products, arithmetic and copies ran while one was open for 0% -> 0% of each run, Pallas kernels for 0% -> 18%
where the time goes in v4:
time: 44.6 us; the launch traced here: 44.2 us
  Pallas kernels  42.8 us (96%)
  starting transfers between devices  0.74 us (2%)
  between operations  0.66 us (1%)
    pallas_call x1, Pallas kernels, attend(): pl.pallas_call(attend_kernel, out_shape=(jax.ShapeDtypeStruct((seq, 4 * H...  31.2 us
    pallas_call x1, Pallas kernels, zero_most(): pl.pallas_call(zero_kernel, out_shape=(jax.ShapeDtypeStruct((experts, seq...  7.95 us
    pallas_call x1, Pallas kernels, dispatch(): pl.pallas_call(dispatch_kernel, out_shape=(jax.ShapeDtypeStruct(buf.shape...  3.65 us
  transfers between devices with their start and end apart: 1, of which 0 were waited for; matrix products, arithmetic and copies ran while one was open for 0% of the time, Pallas kernels for 18%

profile of v4, /device:TPU:0, one launch (start us, length us, event | category | flops | bytes accessed | tf_op | source)
XLA Modules:
  0.0 44.2 jit_solution(6915369397055911198)
XLA Ops:
  0.6 31.2 %attend.1 = (bf16[64,2048]{1,0:T(8,128)(2,1)}, bf16[64,2048]{1,0:T(8,128)(2,1)}, s32[1,256]{1,0:T(1,128)}, f32[8,64]{1,0:T(8,128)}) custom-call(bf16[16,6144]{1,0:T(8,128)(2,1)} %x_hbm.1, s32[2,16]{1,0:T(2,128)} %bitcast.1, f32[16,160]{1,0:T(8,128)} %probs_hbm.1, bf16[6144,12288]{1,0:T(8,128)(2,1)} %wq_hbm.1, bf16[6144,1024]{1,0:T(8,128)(2,1)} %wk_hbm.1, ...), custom_call_target="tpu_custom_call" | custom-call | flops 4831838208 | bytes 82000000 | tf_op jit(solution)/shard_map/attend/pallas_call | solution.py:356
  31.8 0.7 %collective-permute-start = (bf16[64,2048]{1,0:T(8,128)(2,1)}, bf16[64,2048]{1,0:T(8,128)(2,1)}, u32[]{:S(2)}, u32[]{:S(2)}) collective-permute-start(bf16[64,2048]{1,0:T(8,128)(2,1)} %get-tuple-element.14.tail_hbm), channel_id=1, source_target_pairs={{0,2},{1,3},{2,0},{3,1},{4,6},{5,7},{6,4},{7,5}} | collective-permute-start | bytes 786440 | tf_op jit(solution)/shard_map/ppermute | solution.py:550
  32.6 7.9 %zero_most.1 = (bf16[40,64,6144]{2,1,0:T(8,128)(2,1)}, s32[1,256]{1,0:T(1,128)}) custom-call(s32[1,256]{1,0:T(1,128)} %get-tuple-element.10.occ_hbm), custom_call_target="tpu_custom_call" | custom-call | flops 8000000000 | bytes 23592960 | tf_op jit(solution)/shard_map/zero_most/pallas_call | solution.py:413
  40.5 0.0 collective-permute-done.far_hbm
  40.5 3.7 %dispatch.1 = (bf16[40,64,6144]{2,1,0:T(8,128)(2,1)}, bf16[16,6144]{1,0:T(8,128)(2,1)}) custom-call(s32[1,256]{1,0:T(1,128)} %get-tuple-element.11.list_hbm, s32[1,256]{1,0:T(1,128)} %get-tuple-element.10.occ_hbm, f32[8,64]{1,0:T(8,128)} %get-tuple-element.12.prep_hbm, bf16[64,2048]{1,0:T(8,128)(2,1)} %get-tuple-element.13.head_hbm, ...), custom_call_target="tpu_custom_call", output_to_operand_aliasing={{0}: (6, {})} | custom-call | flops 4000000000 | bytes 15728640 | tf_op jit(solution)/shard_map/dispatch/pallas_call | solution.py:528
Async XLA Ops:
  31.8 8.7 %collective-permute-start = (bf16[64,2048]{1,0:T(8,128)(2,1)}, bf16[64,2048]{1,0:T(8,128)(2,1)}, u32[]{:S(2)}, u32[]{:S(2)}) collective-permute-start(bf16[64,2048]{1,0:T(8,128)(2,1)} %get-tuple-element.14.tail_hbm), channel_id=1, source_target_pairs={{0,2},{1,3},{2,0},{3,1},{4,6},{5,7},{6,4},{7,5}} | collective-permute-start | bytes 786440 | tf_op jit(solution)/shard_map/ppermute | solution.py:550

commit v5 on v4

--- a/solution.py
+++ b/solution.py
@@ -12,8 +12,9 @@
 PARTS = ((0, 512), (512, 512), (1024, 512))
 HEAD = 512
 SEGS = ((0, 1536), (0, 1024), (1024, 512))
-EARLY = 4
-ZERO_FIRST = 30
+EARLY = 3
+ZERO_FIRST = 31
+BLIND = 4
 BLOCKS = 8
 OCC = 256
 PLACE = (8, 9, 0, 1, 2, 3, 4, 5)
@@ -90,10 +91,12 @@
             wo_hbm.at[span((peer_of(me, i % 4) * 2 + i // 4) * wide, wide), pl.ds(pl.multiple_of(me * wide + off, 128), size)],
             ring.at[pl.ds(PLACE[i] * wide, wide), pl.ds(off, size)], p_sem.at[p_sem_at(p, i)])
 
-    def p_dot(p, i, count):
+    def p_dot(p, i, count, waits=None):
         off, size = PARTS[p]
-        tile = ring.at[pl.ds(PLACE[i] * wide, count * wide), pl.ds(off, size)]
-        pltpu.make_async_copy(wo_hbm.at[pl.ds(0, count * wide), pl.ds(0, size)], tile, p_sem.at[p_sem_at(p, i)]).wait()
+        waits = count if waits is None else waits
+        if waits:
+            tile = ring.at[pl.ds(PLACE[i] * wide, waits * wide), pl.ds(off, size)]
+            pltpu.make_async_copy(wo_hbm.at[pl.ds(0, waits * wide), pl.ds(0, size)], tile, p_sem.at[p_sem_at(p, i)]).wait()
         base = PLACE[i] * wide
         part = dot(o_all[:, i * wide:(i + count) * wide], ring[base:base + count * wide, off:off + size])
         if i == 0:
@@ -308,11 +311,13 @@
     p_dot(1, 2, 4)
     o_far(2).wait_recv()
     o_pass(2).start()
+    p_dot(0, 6, 1, 2)
+    p_dot(1, 6, 1, 2)
     o_pass(1).wait_recv()
     o_pass(2).wait_recv()
-    p_dot(0, 6, 2)
+    p_dot(0, 7, 1, 0)
     finish(0)
-    p_dot(1, 6, 2)
+    p_dot(1, 7, 1, 0)
     finish(1)
     p_dot(2, 0, 2)
     p_dot(2, 2, 4)
@@ -382,14 +387,36 @@
     )(x, ids_t, probs, w_q, w_k, w_v, w_o)
 
 
-def zero_kernel(occ_hbm, buf_hbm, list_hbm, occ_ref, list_ref, zero, z_sem, io_sem):
+def zero_kernel(occ_hbm, buf_hbm, list_hbm, occ_ref, list_ref, zero, e_sem, z_sem, io_sem):
     experts = buf_hbm.shape[0]
+    tok = buf_hbm.shape[1] // 4
     occ_copy = pltpu.make_async_copy(occ_hbm, occ_ref, io_sem.at[0])
     list_copy = pltpu.make_async_copy(list_ref, list_hbm, io_sem.at[1])
     occ_copy.start()
     zero[...] = jnp.zeros_like(zero)
-    lax.fori_loop(0, ZERO_FIRST, lambda e, c: (pltpu.make_async_copy(zero, buf_hbm.at[e], z_sem).start(), c)[1], 0)
+    lax.fori_loop(0, BLIND, lambda e, c: (pltpu.make_async_copy(zero, buf_hbm.at[e], e_sem).start(), c)[1], 0)
     occ_copy.wait()
+
+    def fill(e, wait):
+        ones = [occ_ref[0, e * 4 + i] for i in range(4)]
+        used = ones[0] + ones[1] + ones[2] + ones[3]
+
+        def move(src, dst):
+            copy = pltpu.make_async_copy(src, dst, z_sem)
+            copy.wait() if wait else copy.start()
+
+        @pl.when(used == 0)
+        def _():
+            move(zero, buf_hbm.at[e])
+
+        @pl.when(used != 0)
+        def _():
+            for i in range(4):
+                @pl.when(ones[i] == 0)
+                def _():
+                    move(zero.at[pl.ds(0, tok)], buf_hbm.at[e, pl.ds(i * tok, tok)])
+
+    lax.fori_loop(BLIND, ZERO_FIRST, lambda e, c: (fill(e, False), c)[1], 0)
 
     def expert(e, count):
         for i in range(4):
@@ -403,8 +430,9 @@
 
     list_ref[0, OCC - 1] = lax.fori_loop(0, experts, expert, 0)
     list_copy.start()
-    filled = buf_hbm.at[pl.ds(0, ZERO_FIRST)]
-    pltpu.make_async_copy(filled, filled, z_sem).wait()
+    filled = buf_hbm.at[pl.ds(0, BLIND)]
+    pltpu.make_async_copy(filled, filled, e_sem).wait()
+    lax.fori_loop(BLIND, ZERO_FIRST, lambda e, c: (fill(e, True), c)[1], 0)
     list_copy.wait()
 
 
@@ -416,7 +444,7 @@
         in_specs=[ANY],
         out_specs=(ANY, ANY),
         scratch_shapes=[pltpu.SMEM((1, OCC), jnp.int32), pltpu.SMEM((1, OCC), jnp.int32), pltpu.VMEM((seq, width), BF16),
-                        dma, dma((2,))],
+                        dma, dma, dma((2,))],
         compiler_params=pltpu.CompilerParams(vmem_limit_bytes=67_043_328),
         cost_estimate=pl.CostEstimate(flops=8_000_000_000, bytes_accessed=ZERO_FIRST * seq * width * 2, transcendentals=0),
         name='zero_most',
@@ -445,8 +473,7 @@
             cut = pl.ds(pl.multiple_of((chip * 2 + core) * wide + HEAD, 512), rest)
             pltpu.make_async_copy(src.at[:, pl.ds(core * rest, rest)], h.at[:, cut], h_sem).start()
     zero[...] = jnp.zeros_like(zero)
-    for e in range(ZERO_FIRST, settled):
-        pltpu.make_async_copy(zero, buf_hbm.at[e], e_sem).start()
+    lax.fori_loop(ZERO_FIRST, settled, lambda e, c: (pltpu.make_async_copy(zero, buf_hbm.at[e], e_sem).start(), c)[1], 0)
     list_copy.wait()
     occ_copy.wait()
 

time: 44.6 us -> 44.3 us (level)
  transfers between devices with their start and end apart: 1 -> 1, of which waited for: 0 -> 1; matrix products, arithmetic and copies ran while one was open for 0% -> 0% of each run, Pallas kernels for 18% -> 18%
where the time goes in v5:
time: 44.3 us; the launch traced here: 43.7 us
  Pallas kernels  42.4 us (96%)
  starting transfers between devices  0.67 us (2%)
  between operations  0.65 us (1%)
    pallas_call x1, Pallas kernels, attend(): pl.pallas_call(attend_kernel, out_shape=(jax.ShapeDtypeStruct((seq, 4 * H...  30.9 us
    pallas_call x1, Pallas kernels, zero_most(): pl.pallas_call(zero_kernel, out_shape=(jax.ShapeDtypeStruct((experts, seq...  7.9 us
    pallas_call x1, Pallas kernels, dispatch(): pl.pallas_call(dispatch_kernel, out_shape=(jax.ShapeDtypeStruct(buf.shape...  3.55 us
  transfers between devices with their start and end apart: 1, of which 1 were waited for; matrix products, arithmetic and copies ran while one was open for 0% of the time, Pallas kernels for 18%

profile of v5, /device:TPU:0, one launch (start us, length us, event | category | flops | bytes accessed | tf_op | source)
XLA Modules:
  0.0 43.7 jit_solution(6774443134305408825)
XLA Ops:
  0.6 30.9 %attend.1 = (bf16[64,2048]{1,0:T(8,128)(2,1)}, bf16[64,2048]{1,0:T(8,128)(2,1)}, s32[1,256]{1,0:T(1,128)}, f32[8,64]{1,0:T(8,128)}) custom-call(bf16[16,6144]{1,0:T(8,128)(2,1)} %x_hbm.1, s32[2,16]{1,0:T(2,128)} %bitcast.1, f32[16,160]{1,0:T(8,128)} %probs_hbm.1, bf16[6144,12288]{1,0:T(8,128)(2,1)} %wq_hbm.1, bf16[6144,1024]{1,0:T(8,128)(2,1)} %wk_hbm.1, ...), custom_call_target="tpu_custom_call" | custom-call | flops 4831838208 | bytes 82000000 | tf_op jit(solution)/shard_map/attend/pallas_call | solution.py:361
  31.5 0.7 %collective-permute-start = (bf16[64,2048]{1,0:T(8,128)(2,1)}, bf16[64,2048]{1,0:T(8,128)(2,1)}, u32[]{:S(2)}, u32[]{:S(2)}) collective-permute-start(bf16[64,2048]{1,0:T(8,128)(2,1)} %get-tuple-element.14.tail_hbm), channel_id=1, source_target_pairs={{0,2},{1,3},{2,0},{3,1},{4,6},{5,7},{6,4},{7,5}} | collective-permute-start | bytes 786440 | tf_op jit(solution)/shard_map/ppermute | solution.py:577
  32.2 7.9 %zero_most.1 = (bf16[40,64,6144]{2,1,0:T(8,128)(2,1)}, s32[1,256]{1,0:T(1,128)}) custom-call(s32[1,256]{1,0:T(1,128)} %get-tuple-element.10.occ_hbm), custom_call_target="tpu_custom_call" | custom-call | flops 8000000000 | bytes 24379392 | tf_op jit(solution)/shard_map/zero_most/pallas_call | solution.py:441
  40.1 0.1 collective-permute-done.far_hbm
  40.2 3.6 %dispatch.1 = (bf16[40,64,6144]{2,1,0:T(8,128)(2,1)}, bf16[16,6144]{1,0:T(8,128)(2,1)}) custom-call(s32[1,256]{1,0:T(1,128)} %get-tuple-element.11.list_hbm, s32[1,256]{1,0:T(1,128)} %get-tuple-element.10.occ_hbm, f32[8,64]{1,0:T(8,128)} %get-tuple-element.12.prep_hbm, bf16[64,2048]{1,0:T(8,128)(2,1)} %get-tuple-element.13.head_hbm, ...), custom_call_target="tpu_custom_call", output_to_operand_aliasing={{0}: (6, {})} | custom-call | flops 4000000000 | bytes 15728640 | tf_op jit(solution)/shard_map/dispatch/pallas_call | solution.py:555
Async XLA Ops:
  31.5 8.6 %collective-permute-start = (bf16[64,2048]{1,0:T(8,128)(2,1)}, bf16[64,2048]{1,0:T(8,128)(2,1)}, u32[]{:S(2)}, u32[]{:S(2)}) collective-permute-start(bf16[64,2048]{1,0:T(8,128)(2,1)} %get-tuple-element.14.tail_hbm), channel_id=1, source_target_pairs={{0,2},{1,3},{2,0},{3,1},{4,6},{5,7},{6,4},{7,5}} | collective-permute-start | bytes 786440 | tf_op jit(solution)/shard_map/ppermute | solution.py:577

commit v6 on v5

--- a/solution.py
+++ b/solution.py
@@ -13,7 +13,7 @@
 HEAD = 512
 SEGS = ((0, 1536), (0, 1024), (1024, 512))
 EARLY = 3
-ZERO_FIRST = 31
+ZERO_FIRST = 30
 BLIND = 4
 BLOCKS = 8
 OCC = 256

time: 44.3 us -> 44 us (level)
  no operation moved by 1% of the time
where the time goes in v6:
time: 44 us; the launch traced here: 43.8 us
  Pallas kernels  42.3 us (96%)
  starting transfers between devices  0.67 us (2%)
  between operations  0.65 us (1%)
    pallas_call x1, Pallas kernels, attend(): pl.pallas_call(attend_kernel, out_shape=(jax.ShapeDtypeStruct((seq, 4 * H...  30.9 us
    pallas_call x1, Pallas kernels, zero_most(): pl.pallas_call(zero_kernel, out_shape=(jax.ShapeDtypeStruct((experts, seq...  7.78 us
    pallas_call x1, Pallas kernels, dispatch(): pl.pallas_call(dispatch_kernel, out_shape=(jax.ShapeDtypeStruct(buf.shape...  3.61 us
  transfers between devices with their start and end apart: 1, of which 1 were waited for; matrix products, arithmetic and copies ran while one was open for 0% of the time, Pallas kernels for 18%

profile of v6, /device:TPU:0, one launch (start us, length us, event | category | flops | bytes accessed | tf_op | source)
XLA Modules:
  0.0 43.8 jit_solution(8613988490908998047)
XLA Ops:
  0.6 30.9 %attend.1 = (bf16[64,2048]{1,0:T(8,128)(2,1)}, bf16[64,2048]{1,0:T(8,128)(2,1)}, s32[1,256]{1,0:T(1,128)}, f32[8,64]{1,0:T(8,128)}) custom-call(bf16[16,6144]{1,0:T(8,128)(2,1)} %x_hbm.1, s32[2,16]{1,0:T(2,128)} %bitcast.1, f32[16,160]{1,0:T(8,128)} %probs_hbm.1, bf16[6144,12288]{1,0:T(8,128)(2,1)} %wq_hbm.1, bf16[6144,1024]{1,0:T(8,128)(2,1)} %wk_hbm.1, ...), custom_call_target="tpu_custom_call" | custom-call | flops 4831838208 | bytes 82000000 | tf_op jit(solution)/shard_map/attend/pallas_call | solution.py:361
  31.5 0.7 %collective-permute-start = (bf16[64,2048]{1,0:T(8,128)(2,1)}, bf16[64,2048]{1,0:T(8,128)(2,1)}, u32[]{:S(2)}, u32[]{:S(2)}) collective-permute-start(bf16[64,2048]{1,0:T(8,128)(2,1)} %get-tuple-element.14.tail_hbm), channel_id=1, source_target_pairs={{0,2},{1,3},{2,0},{3,1},{4,6},{5,7},{6,4},{7,5}} | collective-permute-start | bytes 786440 | tf_op jit(solution)/shard_map/ppermute | solution.py:577
  32.2 7.8 %zero_most.1 = (bf16[40,64,6144]{2,1,0:T(8,128)(2,1)}, s32[1,256]{1,0:T(1,128)}) custom-call(s32[1,256]{1,0:T(1,128)} %get-tuple-element.10.occ_hbm), custom_call_target="tpu_custom_call" | custom-call | flops 8000000000 | bytes 23592960 | tf_op jit(solution)/shard_map/zero_most/pallas_call | solution.py:441
  40.0 0.2 collective-permute-done.far_hbm
  40.2 3.6 %dispatch.1 = (bf16[40,64,6144]{2,1,0:T(8,128)(2,1)}, bf16[16,6144]{1,0:T(8,128)(2,1)}) custom-call(s32[1,256]{1,0:T(1,128)} %get-tuple-element.11.list_hbm, s32[1,256]{1,0:T(1,128)} %get-tuple-element.10.occ_hbm, f32[8,64]{1,0:T(8,128)} %get-tuple-element.12.prep_hbm, bf16[64,2048]{1,0:T(8,128)(2,1)} %get-tuple-element.13.head_hbm, ...), custom_call_target="tpu_custom_call", output_to_operand_aliasing={{0}: (6, {})} | custom-call | flops 4000000000 | bytes 15728640 | tf_op jit(solution)/shard_map/dispatch/pallas_call | solution.py:555
Async XLA Ops:
  31.5 8.6 %collective-permute-start = (bf16[64,2048]{1,0:T(8,128)(2,1)}, bf16[64,2048]{1,0:T(8,128)(2,1)}, u32[]{:S(2)}, u32[]{:S(2)}) collective-permute-start(bf16[64,2048]{1,0:T(8,128)(2,1)} %get-tuple-element.14.tail_hbm), channel_id=1, source_target_pairs={{0,2},{1,3},{2,0},{3,1},{4,6},{5,7},{6,4},{7,5}} | collective-permute-start | bytes 786440 | tf_op jit(solution)/shard_map/ppermute | solution.py:577
